TPU v7x, 32 devices: a 4x4x1 block of a 4x4x8 slice. The times are simulated.
32 devices in a mesh: dp: 1 (over z), ri: 4 (over y), co: 4 (over x), ro: 2 (over core).
Axes of the slice: x: 4, y: 4, z: 1, core: 2. Of those that a mesh axis runs over, the one named last changes fastest.
The devices are a block of a 4x4x8 slice.
Arguments:
- x_act: bfloat16 [16384, 4096], P(('dp', 'ro', 'ri'), 'co')
- w_proj: bfloat16 [4096, 14336], P(('ro', 'ri'), 'co')
- grad_out: bfloat16 [16384, 14336], P(('dp', 'ro', 'ri'), 'co')
Outputs:
- output 1: bfloat16 [16384, 4096], P(('dp', 'ro', 'ri'), 'co')
- output 2: float32 [4096, 14336], P(('dp', 'ro', 'ri'), 'co')
All inputs are finite; a program needn't handle non-finite values.
Results may differ from a plain program's by a relative error of at most 0.001.
Values are sent between devices in bfloat16 or wider.
A program may use at most 768 MiB of HBM per device.

v0:
```python
import jax
import jax.numpy as jnp
from jax import lax
from jax.sharding import PartitionSpec as P


def solution(mesh):
    row_axes = ("ro", "ri")
    spec_act = P(("dp", "ro", "ri"), "co")
    spec_w = P(("ro", "ri"), "co")

    def local_step(x_blk, w_blk, g_blk):
        w_cols = lax.all_gather(w_blk, row_axes, axis=0, tiled=True)
        x_rows = lax.all_gather(x_blk, "co", axis=1, tiled=True)
        gx_part = lax.dot_general(g_blk, w_cols, (((1,), (1,)), ((), ())), preferred_element_type=jnp.float32)
        gw_part = lax.dot_general(x_rows, g_blk, (((0,), (0,)), ((), ())), preferred_element_type=jnp.float32)
        grad_x = lax.psum_scatter(gx_part, "co", scatter_dimension=1, tiled=True).astype(jnp.bfloat16)
        grad_w = lax.psum_scatter(gw_part, row_axes, scatter_dimension=0, tiled=True)
        return grad_x, grad_w

    return jax.shard_map(local_step, mesh=mesh, in_specs=(spec_act, spec_w, spec_act), out_specs=(spec_act, spec_act), check_vma=False)
```

profile of v0, /device:TPU:104, one launch (start us, length us, event | category | flops | bytes accessed | tf_op | source)
XLA Modules:
  0.0 1156.3 jit_solution(242952226668119630)
XLA Ops:
  7.2 0.1 all-gather.3.cloned.1.call-start
  7.2 0.7 all-gather.3.cloned.1.call-update
  8.0 0.1 all-gather.5.cloned.1.call-start
  8.0 0.7 all-gather.5.cloned.1.call-update
  8.8 0.1 reduce-scatter.3.cloned.1.call-start
  8.8 139.6 %all-gather.3.cloned.1.call-done = bf16[4096,3584]{1,0:T(8,128)(2,1)} async-done(((bf16[512,3584]{1,0:T(8,128)(2,1)}), bf16[4096,3584]{1,0:T(8,128)(2,1)}) %all-gather.3.cloned.1.call-update) | async-done | bytes 29360144 | tf_op jit(solution)/shard_map/all_gather | solution.py:13
  148.4 71.0 %fusion = f32[2048,4096]{1,0:T(8,128)} fusion(bf16[2048,3584]{1,0:T(8,128)(2,1)} %param.5, bf16[4096,3584]{1,0:T(8,128)(2,1)} %all-gather.3.cloned.1.call-done), kind=kOutput, calls=%fused_computation | convolution fusion | flops 60129542144 | bytes 77594624 | tf_op jit(solution)/shard_map/dot_general | solution.py:15
  219.4 0.1 reduce-scatter.3.cloned.1.call-update
  219.5 0.2 reduce-scatter.5.cloned.1.call-start
  219.7 83.5 %all-gather.5.cloned.1.call-done = bf16[2048,4096]{1,0:T(8,128)(2,1)} async-done(((bf16[2048,1024]{1,0:T(8,128)(2,1)}), bf16[2048,4096]{1,0:T(8,128)(2,1)}) %all-gather.5.cloned.1.call-update) | async-done | bytes 16777232 | tf_op jit(solution)/shard_map/all_gather | solution.py:14
  303.3 70.9 %fusion.1 = f32[4096,3584]{1,0:T(8,128)} fusion(bf16[2048,4096]{1,0:T(8,128)(2,1)} %all-gather.5.cloned.1.call-done, bf16[2048,3584]{1,0:T(8,128)(2,1)} %param.5), kind=kOutput, calls=%fused_computation.1 | convolution fusion | flops 60129542144 | bytes 90177536 | tf_op jit(solution)/shard_map/dot_general | solution.py:16
  374.2 0.1 reduce-scatter.5.cloned.1.call-update
  374.2 212.6 %reduce-scatter.3.cloned.1.call-done = f32[2048,1024]{1,0:T(8,128)} async-done(((f32[2048,4096]{1,0:T(8,128)}), f32[2048,1024]{1,0:T(8,128)}) %reduce-scatter.3.cloned.1.call-update) | async-done | bytes 8388624 | tf_op jit(solution)/shard_map/reduce_scatter | solution.py:17
  586.9 6.1 convert_element_type.3
  592.9 556.8 %reduce-scatter.5.cloned.1.call-done = f32[512,3584]{1,0:T(8,128)} async-done(((f32[4096,3584]{1,0:T(8,128)}), f32[512,3584]{1,0:T(8,128)}) %reduce-scatter.5.cloned.1.call-update) | async-done | bytes 7340048 | tf_op jit(solution)/shard_map/reduce_scatter | solution.py:18
Async XLA Ops:
  7.2 141.2 %all-gather.3.cloned.1.call-start = ((), (), s32[]{:S(2)}) async-start(), calls=%async_computation.2 | async-start | bytes 33030144 | tf_op jit(solution)/shard_map/all_gather | solution.py:13
  8.0 295.3 %all-gather.5.cloned.1.call-start = ((), (), s32[]{:S(2)}) async-start(), calls=%async_computation.4 | async-start | bytes 20971520 | tf_op jit(solution)/shard_map/all_gather | solution.py:14
  8.8 578.1 %reduce-scatter.3.cloned.1.call-start = ((), (), s32[]{:S(2)}) async-start(), calls=%async_computation.3 | async-start | bytes 41943040 | tf_op jit(solution)/shard_map/reduce_scatter | solution.py:17
  219.5 930.2 %reduce-scatter.5.cloned.1.call-start = ((), (), s32[]{:S(2)}) async-start(), calls=%async_computation.5 | async-start | bytes 66060288 | tf_op jit(solution)/shard_map/reduce_scatter | solution.py:18
Sparse Core Ops, SparseCore 0:
  9.6 138.7 all-gather.2
  150.0 153.2 all-gather.4
  305.7 281.1 reduce-scatter.2
  589.7 560.0 reduce-scatter.4
where the time goes:
time: 1160 us
  waiting for transfers between devices  994 us (86%)
  matrix products  142 us (12%)
  between operations  13.8 us (1%)
    reduce_scatter x1, waiting for transfers between devices, local_step(): lax.psum_scatter(gw_part, row_axes, scatter_dimension=0, tiled=True)  557 us
    reduce_scatter x1, waiting for transfers between devices, local_step(): lax.psum_scatter(gx_part, 'co', scatter_dimension=1, tiled=True)  213 us
    all_gather x1, waiting for transfers between devices, local_step(): w_cols = lax.all_gather(w_blk, row_axes, axis=0, tiled=True)  140 us
    all_gather x1, waiting for transfers between devices, local_step(): x_rows = lax.all_gather(x_blk, 'co', axis=1, tiled=True)  83.5 us
    dot_general x1, matrix products, local_step(): lax.dot_general(g_blk, w_cols, (((1,), (1,)), ((), ())), preferred_elemen...  71 us
    dot_general x1, matrix products, local_step(): lax.dot_general(x_rows, g_blk, (((0,), (0,)), ((), ())), preferred_elemen...  70.9 us
  transfers between devices with their start and end apart: 4, of which 4 were waited for; matrix products, arithmetic and copies ran while one was open for 13% of the time, Pallas kernels for 0%

commit v1 on v0

v1 whole, which is shorter than its diff:
```python
import functools

import jax
import jax.numpy as jnp
from jax import lax
from jax.experimental import pallas as pl
from jax.experimental.pallas import tpu as pltpu
from jax.sharding import PartitionSpec as P

MESH = pl.DeviceIdType.MESH
BF16, F32 = jnp.bfloat16, jnp.float32
NC = 8


def kernel(x, w, g, dx, dw, pp, qq, xa, rx, ry, gv, wv,
           loc, d2d, dr, wr, xr, swd, swf, sxd, sxf, sx, rxs, sy, rys, fxs, fxr, fys, fyr, pos, qos, ins, ads):
    h, y, c = lax.axis_index("ro"), lax.axis_index("ri"), lax.axis_index("co")
    o = 1 - h
    tb, dcols = x.shape
    wrows, f = w.shape
    q = wrows // 2
    cr, qr = tb // NC, q // NC
    ft = f // 7
    yn = [lax.rem(y + 1, 4), lax.rem(y + 3, 4)]
    cn = [lax.rem(c + 1, 4), lax.rem(c + 3, 4)]
    y2, c2 = lax.rem(y + 2, 4), lax.rem(c + 2, 4)
    sib = {"ro": o}

    def rc(src, dst, ss, rs, dev):
        return pltpu.make_async_remote_copy(src_ref=src, dst_ref=dst, send_sem=ss, recv_sem=rs, device_id=dev, device_id_type=MESH)

    def lc(src, dst, sem):
        return pltpu.make_async_copy(src, dst, sem)

    def xor(a, b):
        return 2 * lax.rem(a // 2 + b // 2, 2) + lax.rem(lax.rem(a, 2) + lax.rem(b, 2), 2)

    bar = pltpu.get_barrier_semaphore()
    partners = [sib]
    for e in range(2):
        for k in (h, o):
            partners += [{"ri": yn[e], "ro": k}, {"co": cn[e], "ro": k}]
    for dev in partners:
        pl.semaphore_signal(bar, 1, device_id=dev, device_id_type=MESH)
    pl.semaphore_wait(bar, len(partners))

    def xcols(i, k):
        return x.at[:, pl.ds(pl.multiple_of(i * 2 * q + k * q, q), q)]

    def wrow(k):
        return w.at[pl.ds(pl.multiple_of(k * q, q), q)]

    gc = tb // 4
    w_d2d = rc(wrow(o), wv.at[y, h], d2d.at[0], wr.at[y, h], sib)
    g_d2d = [rc(g.at[pl.ds(n * gc, gc)], gv.at[h, pl.ds(n * gc, gc)], d2d.at[1 + n], dr.at[n], sib) for n in range(4)]
    x_d2d = [rc(xcols(i, o), xa.at[c, h, i], d2d.at[5 + i], xr.at[c, h, i], sib) for i in range(2)]
    w_dir, x_dir = [], []
    for n in range(2):
        for e in range(2):
            k = h if n == e else o
            w_dir.append(rc(wrow(k), wv.at[y, h], swd.at[e, n], wr.at[y, h], {"ri": yn[e], "ro": k}))
            for i in range(2):
                x_dir.append(rc(xcols(i, k), xa.at[c, h, i], sxd.at[e, n, i], xr.at[c, h, i], {"co": cn[e], "ro": k}))
    w_loc = lc(wrow(h), wv.at[y, h], loc.at[0])
    g_loc = [lc(g.at[pl.ds(n * gc, gc)], gv.at[h, pl.ds(n * gc, gc)], loc.at[1 + n]) for n in range(4)]
    w_loc.start()
    g_loc[0].start()
    w_d2d.start()
    for cp in w_dir + x_dir:
        cp.start()
    for cp in g_loc[1:] + g_d2d + x_d2d:
        cp.start()

    w_fwd = [rc(wv.at[yn[1 - e], k], wv.at[yn[1 - e], k], swf.at[e], wr.at[yn[1 - e], k], {"ri": yn[e]}) for e, k in ((0, h), (1, o))]
    x_fwd = [rc(xa.at[cn[1 - e], k, i], xa.at[cn[1 - e], k, i], sxf.at[e, i], xr.at[cn[1 - e], k, i], {"co": cn[e]})
             for e, k in ((0, h), (1, o)) for i in range(2)]

    def got_w(yy, k):
        rc(wv.at[yy, k], wv.at[yy, k], swf.at[0], wr.at[yy, k], sib).wait_recv()

    def got_x(cc, k):
        for i in range(2):
            rc(xa.at[cc, k, i], xa.at[cc, k, i], sxf.at[0, i], xr.at[cc, k, i], sib).wait_recv()

    def sends(part, recv, ss, rs, me, axis, nbr, d):
        k = lax.rem(d - me + 4, 4)

        @pl.when(k == 2)
        def _():
            @pl.loop(0, NC)
            def _(j):
                for e in range(2):
                    rc(part.at[d, e, j], recv.at[0, e, j], ss.at[0, e, j], rs.at[0, e, j], {axis: nbr[e]}).start()

        for e in range(2):
            @pl.when(k == 1 + 2 * e)
            def _():
                @pl.loop(0, NC)
                def _(j):
                    rc(part.at[d, 1 - e, j], recv.at[1, e, j], ss.at[1, e, j], rs.at[1, e, j], {axis: nbr[e]}).start()

    x_sends = functools.partial(sends, pp, rx, sx, rxs, c, "co", cn)
    y_sends = functools.partial(sends, qq, ry, sy, rys, y, "ri", yn)

    def compute(xin, xt, pst, qst):
        xo_in = [lc(xcols(i, h), xin.at[i, 0], ins.at[i, 0]) for i in range(2)]
        xo_out = [lc(xin.at[i, 0], xa.at[c, h, i], ins.at[i, 1]) for i in range(2)]
        for cp in xo_in:
            cp.start()

        def p_out(slot, r, yy, m):
            s, ab, hf = 1 - m // 4, lax.rem(m // 2, 2), lax.rem(m, 2)
            return lc(pst.at[slot, r], pp.at[2 * r + yy // 2, ab, pl.ds(s * 4 + hf * 2, 2), :, pl.ds(pl.multiple_of(lax.rem(yy, 2) * q, q), q)], pos.at[slot, r])

        def p_step(yy, first):
            @pl.loop(0, 8)
            def _(m):
                @pl.when(first & (m == 4))
                def _():
                    for n in range(4):
                        rc(g.at[pl.ds(n * gc, gc)], gv.at[o, pl.ds(n * gc, gc)], d2d.at[1 + n], dr.at[n], sib).wait_recv()

                s, ab, hf = 1 - m // 4, lax.rem(m // 2, 2), lax.rem(m, 2)
                t = s * h + (1 - s) * o
                row = pl.multiple_of(ab * (tb // 2) + hf * (tb // 4), tb // 4)
                slot = lax.rem(m, 2)

                @pl.when(m >= 2)
                def _():
                    for r in range(2):
                        p_out(slot, r, yy, m).wait()

                a = gv[t, pl.ds(row, tb // 4), :]
                b = wv[yy].reshape(2 * q, f)
                res = lax.dot_general(a, b, (((1,), (1,)), ((), ())), preferred_element_type=F32)
                for r in range(2):
                    pst[slot, r] = res[:, r * q:(r + 1) * q].reshape(2, cr, q)
                for r in range(2):
                    p_out(slot, r, yy, m).start()

            for slot in range(2):
                for r in range(2):
                    p_out(slot, r, yy, 6 + slot).wait()

        def q_out(slot, r, yy, n):
            s = r * h + (1 - r) * o
            return lc(qst.at[slot, r], qq.at[yy, :, pl.ds(s * 4, 4), :, pl.ds(pl.multiple_of(n * ft, ft), ft)], qos.at[slot, r])

        def q_step(yy):
            cps = [lc(xa.at[2 * r + yy // 2, t, lax.rem(yy, 2)], xin.at[r, t], ins.at[r, t]) for r in range(2) for t in range(2)]
            for cp in cps:
                cp.start()
            for cp in cps:
                cp.wait()

            @pl.loop(0, NC)
            def _(n):
                at = pl.ds(pl.multiple_of(n * cr, cr), cr)
                for r in range(2):
                    for t in range(2):
                        xt[t, r * q:(r + 1) * q, at] = xin[r, t, at, :].T

            @pl.loop(0, 7)
            def _(n):
                slot = lax.rem(n, 2)

                @pl.when(n >= 2)
                def _():
                    for r in range(2):
                        q_out(slot, r, yy, n).wait()

                at = pl.ds(pl.multiple_of(n * ft, ft), ft)
                res = jnp.dot(xt[0], gv[0, :, at], preferred_element_type=F32)
                res += jnp.dot(xt[1], gv[1, :, at], preferred_element_type=F32)
                for r in range(2):
                    qst[slot, r] = res[r * q:(r + 1) * q].reshape(2, 4, qr, ft)
                for r in range(2):
                    q_out(slot, r, yy, n).start()

            for slot in range(2):
                for r in range(2):
                    q_out(slot, r, yy, 0).wait()

        op = lax.rem(y // 2 + c + 1, 2)
        even = 1 - lax.rem(y, 2)
        rem1 = even * h + (1 - even) * o

        @pl.loop(0, 8)
        def _(step):
            @pl.when(step == 0)
            def _():
                w_loc.wait()
                for cp in g_loc:
                    cp.wait()
                got_w(y, o)

            @pl.when(step == 1)
            def _():
                for i in range(2):
                    xo_in[i].wait()
                    xo_out[i].start()
                got_w(yn[1], h)
                w_fwd[0].start()
                got_w(yn[0], o)
                w_fwd[1].start()
                got_x(cn[1], h)
                x_fwd[0].start()
                x_fwd[1].start()
                got_x(cn[0], o)
                x_fwd[2].start()
                x_fwd[3].start()
                got_w(xor(y, 1), rem1)

            @pl.when(step == 2)
            def _():
                x_sends(y // 2)
                x_sends(2 + y // 2)
                got_x(cn[1], o)
                got_x(cn[0], h)
                for i in range(2):
                    xo_out[i].wait()

            @pl.when(step == 3)
            def _():
                got_x(c, o)
                got_x(c2, 0)
                got_x(c2, 1)

            @pl.when(step == 5)
            def _():
                got_w(3 - y, 1 - rem1)

            @pl.when(step == 6)
            def _():
                got_w(y2, 0)
                got_w(y2, 1)

            late = step // 5
            is_p = (step < 2) | ((step >= 5) & (step < 7))
            pn = step - 3 * late
            qn = step - 2 - 2 * (step // 7)
            pcode = pn + pn // 2 - 2 * (pn // 3)
            qa = qn // 2
            qcode = op * ((1 - qa) * (2 + qn) + qa * (3 - qn)) + (1 - op) * lax.rem(qn + 1, 4)

            @pl.when(is_p)
            def _():
                p_step(xor(y, pcode), step == 0)

            @pl.when(jnp.logical_not(is_p))
            def _():
                yy = xor(y, qcode)
                q_step(yy)
                y_sends(yy)

            @pl.when(step == 6)
            def _():
                x_sends(1 - y // 2)
                x_sends(3 - y // 2)

    pl.run_scoped(compute, pltpu.VMEM((2, 2, tb, q), BF16), pltpu.VMEM((2, 2 * q, tb), BF16),
                  pltpu.VMEM((2, 2, 2, cr, q), F32), pltpu.VMEM((2, 2, 2, 4, qr, ft), F32))

    def reduce(ax, ay, bx, by):
        rings = ((pp, rx, sx, rxs, c, cn, "co", ax), (qq, ry, sy, rys, y, yn, "ri", ay))

        @pl.loop(0, NC)
        def _(j):
            for a, (part, recv, ss, rs, me, nbr, axis, buf) in enumerate(rings):
                for e in range(2):
                    rc(recv.at[0, e, j], recv.at[0, e, j], ss.at[0, e, j], rs.at[0, e, j], {axis: nbr[e]}).wait_recv()
                    lc(part.at[nbr[e], e, j], buf.at[e, 0], ads.at[a, e, 0]).start()
                    lc(recv.at[0, e, j], buf.at[e, 1], ads.at[a, e, 1]).start()
            for a, (part, recv, ss, rs, me, nbr, axis, buf) in enumerate(rings):
                for e in range(2):
                    lc(part.at[nbr[e], e, j], buf.at[e, 0], ads.at[a, e, 0]).wait()
                    lc(recv.at[0, e, j], buf.at[e, 1], ads.at[a, e, 1]).wait()
                    buf[e, 2] = buf[e, 0] + buf[e, 1]
                    lc(buf.at[e, 2], part.at[nbr[e], e, j], ads.at[a, e, 2]).start()
            for a, (part, recv, ss, rs, me, nbr, axis, buf) in enumerate(rings):
                for e in range(2):
                    lc(buf.at[e, 2], part.at[nbr[e], e, j], ads.at[a, e, 2]).wait()
                    rc(part.at[nbr[e], e, j], recv.at[2, e, j], ss.at[2, e, j], rs.at[2, e, j], {axis: nbr[e]}).start()

        def x_out(e, j, i, k):
            return dx.at[pl.ds(pl.multiple_of(e * (tb // 2) + lax.rem(j, 4) * cr, cr), cr), pl.ds(pl.multiple_of(i * 2 * q + k * q, q), q)]

        def y_out(e, j, k):
            return dw.at[pl.ds(pl.multiple_of(k * q + e * (q // 2) + lax.rem(j, 4) * qr, qr), qr)]

        def x_rc(e, j, i):
            return rc(bx.at[e, j, :, i * q:(i + 1) * q], x_out(e, j, i, h), fxs.at[e, j, i], fxr.at[e, lax.rem(j, 4), i], sib)

        def x_lc(e, j, i):
            return lc(bx.at[e, j, :, i * q:(i + 1) * q], x_out(e, j, i, h), fxs.at[e, j, i])

        def y_rc(e, j):
            return rc(by.at[e, j], y_out(e, j, h), fys.at[e, j], fyr.at[e, lax.rem(j, 4)], sib)

        def y_lc(e, j):
            return lc(by.at[e, j], y_out(e, j, h), fys.at[e, j])

        @pl.loop(0, NC)
        def _(j):
            for a, (part, recv, ss, rs, me, nbr, axis, buf) in enumerate(rings):
                for e in range(2):
                    rc(recv.at[1, 1 - e, j], recv.at[1, 1 - e, j], ss.at[1, 1 - e, j], rs.at[1, 1 - e, j], {axis: nbr[e]}).wait_recv()
                    lc(part.at[me, e, j], buf.at[e, 0], ads.at[a, e, 0]).start()
                    lc(recv.at[1, 1 - e, j], buf.at[e, 1], ads.at[a, e, 1]).start()
            for a in (1, 0):
                part, recv, ss, rs, me, nbr, axis, buf = rings[a]
                for e in range(2):
                    rc(recv.at[2, e, j], recv.at[2, e, j], ss.at[2, e, j], rs.at[2, e, j], {axis: nbr[e]}).wait_recv()
                    lc(recv.at[2, e, j], buf.at[e, 2], ads.at[a, e, 2]).start()
                for e in range(2):
                    lc(part.at[me, e, j], buf.at[e, 0], ads.at[a, e, 0]).wait()
                    lc(recv.at[1, 1 - e, j], buf.at[e, 1], ads.at[a, e, 1]).wait()
                    lc(recv.at[2, e, j], buf.at[e, 2], ads.at[a, e, 2]).wait()
                    tot = buf[e, 0] + buf[e, 1] + buf[e, 2]
                    if a == 0:
                        bx[e, j] = tot.astype(BF16)
                    else:
                        by[e, j] = tot

                    @pl.when(j < 4)
                    def _():
                        if a == 0:
                            for i in range(2):
                                x_rc(e, j, i).start()
                        else:
                            y_rc(e, j).start()

                    @pl.when(j >= 4)
                    def _():
                        if a == 0:
                            for i in range(2):
                                x_lc(e, j, i).start()
                        else:
                            y_lc(e, j).start()

        @pl.loop(0, NC)
        def _(j):
            for a, (part, recv, ss, rs, me, nbr, axis, buf) in enumerate(rings):
                for e in range(2):
                    for n in range(3):
                        rc(part.at[me, e, j], recv.at[n, e, j], ss.at[n, e, j], rs.at[n, e, j], {axis: nbr[e]}).wait_send()
            for e in range(2):
                @pl.when(j < 4)
                def _():
                    for i in range(2):
                        x_rc(e, j, i).wait()
                    y_rc(e, j).wait()

                @pl.when(j >= 4)
                def _():
                    for i in range(2):
                        x_lc(e, j, i).wait()
                    y_lc(e, j).wait()

        for cp in [w_d2d] + g_d2d + x_d2d + w_dir + x_dir + w_fwd + x_fwd:
            cp.wait_send()

    pl.run_scoped(reduce, pltpu.VMEM((2, 3, cr, 2 * q), F32), pltpu.VMEM((2, 3, qr, f), F32),
                  pltpu.VMEM((2, NC, cr, 2 * q), BF16), pltpu.VMEM((2, NC, qr, f), F32))


def solution(mesh):
    spec_act = P(("dp", "ro", "ri"), "co")
    spec_w = P(("ro", "ri"), "co")

    def local_step(x, w, g):
        tb, dcols = x.shape
        wrows, f = w.shape
        q = wrows // 2
        cr, qr = tb // NC, q // NC
        dma = lambda *s: pltpu.SemaphoreType.DMA(s)
        any_ = pl.BlockSpec(memory_space=pl.ANY)
        shapes = [
            jax.ShapeDtypeStruct((tb, dcols), BF16),
            jax.ShapeDtypeStruct((wrows, f), F32),
            jax.ShapeDtypeStruct((4, 2, NC, cr, 2 * q), F32),
            jax.ShapeDtypeStruct((4, 2, NC, qr, f), F32),
            jax.ShapeDtypeStruct((4, 2, 2, tb, q), BF16),
            jax.ShapeDtypeStruct((3, 2, NC, cr, 2 * q), F32),
            jax.ShapeDtypeStruct((3, 2, NC, qr, f), F32),
        ]
        res = pl.pallas_call(
            kernel,
            out_shape=shapes,
            in_specs=[any_] * 3,
            out_specs=[any_] * len(shapes),
            scratch_shapes=[
                pltpu.VMEM((2, tb, f), BF16),
                pltpu.VMEM((4, 2, q, f), BF16),
                dma(5), dma(7), dma(4), dma(4, 2), dma(4, 2, 2), dma(2, 2), dma(2), dma(2, 2, 2), dma(2, 2),
                dma(3, 2, NC), dma(3, 2, NC), dma(3, 2, NC), dma(3, 2, NC),
                dma(2, NC, 2), dma(2, 4, 2), dma(2, NC), dma(2, 4), dma(2, 2), dma(2, 2), dma(2, 2), dma(2, 2, 3),
            ],
            compiler_params=pltpu.CompilerParams(collective_id=0, has_side_effects=True, vmem_limit_bytes=67043328),
            name="linear_grads",
        )(x, w, g)
        return res[0], res[1]

    return jax.shard_map(local_step, mesh=mesh, in_specs=(spec_act, spec_w, spec_act), out_specs=(spec_act, spec_act), check_vma=False)
```

time: 1160 us -> 432 us (0.37)
  waiting for transfers between devices: 994 us -> 0 us
  Pallas kernels: 0 us -> 416 us
  matrix products: 142 us -> 0 us
  between operations: 13.8 us -> 0.64 us
    reduce_scatter x2 -> x0, waiting for transfers between devices: 769 us -> none  [the longest x1 557 us: local_step(): lax.psum_scatter(gw_part, row_axes, scatter_dimension=0, tiled=True)]
    pallas_call x0 -> x1, Pallas kernels: none -> 416 us  [local_step(): pl.pallas_call(kernel, out_shape=shapes, in_specs=[any_] * 3, out_specs=[...]
    all_gather x2 -> x0, waiting for transfers between devices: 223 us -> none  [the longest x1 140 us: local_step(): w_cols = lax.all_gather(w_blk, row_axes, axis=0, tiled=True)]
    dot_general x2 -> x0, matrix products: 142 us -> none  [the longest x1 71 us: local_step(): lax.dot_general(g_blk, w_cols, (((1,), (1,)), ((), ())), preferred_elemen...]
  transfers between devices with their start and end apart: 4 -> 0, of which waited for: 4 -> 0; matrix products, arithmetic and copies ran while one was open for 13% -> 0% of each run, Pallas kernels for 0% -> 0%
where the time goes in v1:
time: 432 us; the launch traced here: 428 us
  Pallas kernels  416 us (96%)
  local copies, waits for them, and re-layouts  11.2 us (3%)
    pallas_call x1, Pallas kernels, local_step(): pl.pallas_call(kernel, out_shape=shapes, in_specs=[any_] * 3, out_specs=[...  416 us
    unnamed x2, local copies, waits for them, and re-layouts  11.2 us

profile of v1, /device:TPU:104, one launch (start us, length us, event | category | flops | bytes accessed | tf_op | source)
XLA Modules:
  0.0 427.9 jit_solution(11253314099401437617)
XLA Ops:
  0.6 416.1 %linear_grads.1 = (bf16[2048,1024]{1,0:T(8,128)(2,1)}, f32[512,3584]{1,0:T(8,128)}, f32[4,2,8,256,512]{4,3,2,1,0:T(8,128)}, f32[4,2,8,32,3584]{4,3,2,1,0:T(8,128...) custom-call(bf16[2048,1024]{1,0:T(8,128)(2,1)} %x.1, ...), custom_call_target="tpu_custom_call" | custom-call | tf_op jit(solution)/shard_map/linear_grads/pallas_call | solution.py:387
  416.7 4.6 %copy.7 = bf16[2048,1024]{1,0:T(8,128)(2,1)} copy(bf16[2048,1024]{1,0:T(8,128)(2,1)} %get-tuple-element.8) | data formatting | bytes 8388608
  421.3 6.6 %copy.8 = f32[512,3584]{1,0:T(8,128)} copy(f32[512,3584]{1,0:T(8,128)} %get-tuple-element.9) | data formatting | bytes 14680064

commit v2 on v1

--- a/solution.py
+++ b/solution.py
@@ -12,8 +12,8 @@
 NC = 8
 
 
-def kernel(x, w, g, dx, dw, pp, qq, xa, rx, ry, gv, wv,
-           loc, d2d, dr, wr, xr, swd, swf, sxd, sxf, sx, rxs, sy, rys, fxs, fxr, fys, fyr, pos, qos, ins, ads):
+def kernel(x, w, g, dx, dw, pp, qq, xa, wa, rx, ry, gv,
+           loc, d2d, dr, wr, xr, swd, swf, sxd, sxf, sx, rxs, sy, rys, fxs, fxr, fys, fyr, pos, qos, ins, wis, ads):
     h, y, c = lax.axis_index("ro"), lax.axis_index("ri"), lax.axis_index("co")
     o = 1 - h
     tb, dcols = x.shape
@@ -51,19 +51,17 @@
         return w.at[pl.ds(pl.multiple_of(k * q, q), q)]
 
     gc = tb // 4
-    w_d2d = rc(wrow(o), wv.at[y, h], d2d.at[0], wr.at[y, h], sib)
+    w_d2d = rc(wrow(o), wa.at[y, h], d2d.at[0], wr.at[y, h], sib)
     g_d2d = [rc(g.at[pl.ds(n * gc, gc)], gv.at[h, pl.ds(n * gc, gc)], d2d.at[1 + n], dr.at[n], sib) for n in range(4)]
     x_d2d = [rc(xcols(i, o), xa.at[c, h, i], d2d.at[5 + i], xr.at[c, h, i], sib) for i in range(2)]
     w_dir, x_dir = [], []
     for n in range(2):
         for e in range(2):
             k = h if n == e else o
-            w_dir.append(rc(wrow(k), wv.at[y, h], swd.at[e, n], wr.at[y, h], {"ri": yn[e], "ro": k}))
+            w_dir.append(rc(wrow(k), wa.at[y, h], swd.at[e, n], wr.at[y, h], {"ri": yn[e], "ro": k}))
             for i in range(2):
                 x_dir.append(rc(xcols(i, k), xa.at[c, h, i], sxd.at[e, n, i], xr.at[c, h, i], {"co": cn[e], "ro": k}))
-    w_loc = lc(wrow(h), wv.at[y, h], loc.at[0])
     g_loc = [lc(g.at[pl.ds(n * gc, gc)], gv.at[h, pl.ds(n * gc, gc)], loc.at[1 + n]) for n in range(4)]
-    w_loc.start()
     g_loc[0].start()
     w_d2d.start()
     for cp in w_dir + x_dir:
@@ -71,12 +69,12 @@
     for cp in g_loc[1:] + g_d2d + x_d2d:
         cp.start()
 
-    w_fwd = [rc(wv.at[yn[1 - e], k], wv.at[yn[1 - e], k], swf.at[e], wr.at[yn[1 - e], k], {"ri": yn[e]}) for e, k in ((0, h), (1, o))]
+    w_fwd = [rc(wa.at[yn[1 - e], k], wa.at[yn[1 - e], k], swf.at[e], wr.at[yn[1 - e], k], {"ri": yn[e]}) for e, k in ((0, h), (1, o))]
     x_fwd = [rc(xa.at[cn[1 - e], k, i], xa.at[cn[1 - e], k, i], sxf.at[e, i], xr.at[cn[1 - e], k, i], {"co": cn[e]})
              for e, k in ((0, h), (1, o)) for i in range(2)]
 
     def got_w(yy, k):
-        rc(wv.at[yy, k], wv.at[yy, k], swf.at[0], wr.at[yy, k], sib).wait_recv()
+        rc(wa.at[yy, k], wa.at[yy, k], swf.at[0], wr.at[yy, k], sib).wait_recv()
 
     def got_x(cc, k):
         for i in range(2):
@@ -102,7 +100,7 @@
     x_sends = functools.partial(sends, pp, rx, sx, rxs, c, "co", cn)
     y_sends = functools.partial(sends, qq, ry, sy, rys, y, "ri", yn)
 
-    def compute(xin, xt, pst, qst):
+    def compute(wv, xin, xt, pst, qst):
         xo_in = [lc(xcols(i, h), xin.at[i, 0], ins.at[i, 0]) for i in range(2)]
         xo_out = [lc(xin.at[i, 0], xa.at[c, h, i], ins.at[i, 1]) for i in range(2)]
         for cp in xo_in:
@@ -113,6 +111,23 @@
             return lc(pst.at[slot, r], pp.at[2 * r + yy // 2, ab, pl.ds(s * 4 + hf * 2, 2), :, pl.ds(pl.multiple_of(lax.rem(yy, 2) * q, q), q)], pos.at[slot, r])
 
         def p_step(yy, first):
+            cps = [lc(wa.at[yy, r], wv.at[pl.ds(r * q, q)], wis.at[r]) for r in range(2)]
+            w_own = lc(wrow(h), wv.at[pl.ds(pl.multiple_of(h * q, q), q)], wis.at[h])
+            w_oth = lc(wa.at[yy, o], wv.at[pl.ds(pl.multiple_of(o * q, q), q)], wis.at[o])
+
+            @pl.when(first)
+            def _():
+                w_own.start()
+                w_oth.start()
+
+            @pl.when(jnp.logical_not(first))
+            def _():
+                for cp in cps:
+                    cp.start()
+
+            for cp in cps:
+                cp.wait()
+
             @pl.loop(0, 8)
             def _(m):
                 @pl.when(first & (m == 4))
@@ -131,8 +146,7 @@
                         p_out(slot, r, yy, m).wait()
 
                 a = gv[t, pl.ds(row, tb // 4), :]
-                b = wv[yy].reshape(2 * q, f)
-                res = lax.dot_general(a, b, (((1,), (1,)), ((), ())), preferred_element_type=F32)
+                res = lax.dot_general(a, wv[...], (((1,), (1,)), ((), ())), preferred_element_type=F32)
                 for r in range(2):
                     pst[slot, r] = res[:, r * q:(r + 1) * q].reshape(2, cr, q)
                 for r in range(2):
@@ -189,7 +203,6 @@
         def _(step):
             @pl.when(step == 0)
             def _():
-                w_loc.wait()
                 for cp in g_loc:
                     cp.wait()
                 got_w(y, o)
@@ -258,7 +271,7 @@
                 x_sends(1 - y // 2)
                 x_sends(3 - y // 2)
 
-    pl.run_scoped(compute, pltpu.VMEM((2, 2, tb, q), BF16), pltpu.VMEM((2, 2 * q, tb), BF16),
+    pl.run_scoped(compute, pltpu.VMEM((2 * q, f), BF16), pltpu.VMEM((2, 2, tb, q), BF16), pltpu.VMEM((2, 2 * q, tb), BF16),
                   pltpu.VMEM((2, 2, 2, cr, q), F32), pltpu.VMEM((2, 2, 2, 4, qr, ft), F32))
 
     def reduce(ax, ay, bx, by):
@@ -282,23 +295,17 @@
                     lc(buf.at[e, 2], part.at[nbr[e], e, j], ads.at[a, e, 2]).wait()
                     rc(part.at[nbr[e], e, j], recv.at[2, e, j], ss.at[2, e, j], rs.at[2, e, j], {axis: nbr[e]}).start()
 
-        def x_out(e, j, i, k):
-            return dx.at[pl.ds(pl.multiple_of(e * (tb // 2) + lax.rem(j, 4) * cr, cr), cr), pl.ds(pl.multiple_of(i * 2 * q + k * q, q), q)]
-
-        def y_out(e, j, k):
-            return dw.at[pl.ds(pl.multiple_of(k * q + e * (q // 2) + lax.rem(j, 4) * qr, qr), qr)]
+        def x_at(e, j, i):
+            return (pl.ds(pl.multiple_of(e * (tb // 2) + lax.rem(j, 4) * cr, cr), cr), pl.ds(pl.multiple_of(i * 2 * q + h * q, q), q))
+
+        def y_at(e, j):
+            return pl.ds(pl.multiple_of(h * q + e * (q // 2) + lax.rem(j, 4) * qr, qr), qr)
 
         def x_rc(e, j, i):
-            return rc(bx.at[e, j, :, i * q:(i + 1) * q], x_out(e, j, i, h), fxs.at[e, j, i], fxr.at[e, lax.rem(j, 4), i], sib)
-
-        def x_lc(e, j, i):
-            return lc(bx.at[e, j, :, i * q:(i + 1) * q], x_out(e, j, i, h), fxs.at[e, j, i])
+            return rc(bx.at[e, j, :, i * q:(i + 1) * q], dx.at[x_at(e, j, i)], fxs.at[e, j, i], fxr.at[e, j, i], sib)
 
         def y_rc(e, j):
-            return rc(by.at[e, j], y_out(e, j, h), fys.at[e, j], fyr.at[e, lax.rem(j, 4)], sib)
-
-        def y_lc(e, j):
-            return lc(by.at[e, j], y_out(e, j, h), fys.at[e, j])
+            return rc(by.at[e, j], dw.at[y_at(e, j)], fys.at[e, j], fyr.at[e, j], sib)
 
         @pl.loop(0, NC)
         def _(j):
@@ -317,26 +324,24 @@
                     lc(recv.at[1, 1 - e, j], buf.at[e, 1], ads.at[a, e, 1]).wait()
                     lc(recv.at[2, e, j], buf.at[e, 2], ads.at[a, e, 2]).wait()
                     tot = buf[e, 0] + buf[e, 1] + buf[e, 2]
-                    if a == 0:
-                        bx[e, j] = tot.astype(BF16)
-                    else:
-                        by[e, j] = tot
 
                     @pl.when(j < 4)
                     def _():
                         if a == 0:
+                            bx[e, j] = tot.astype(BF16)
                             for i in range(2):
                                 x_rc(e, j, i).start()
                         else:
+                            by[e, j] = tot
                             y_rc(e, j).start()
 
                     @pl.when(j >= 4)
                     def _():
                         if a == 0:
                             for i in range(2):
-                                x_lc(e, j, i).start()
+                                dx[x_at(e, j, i)] = tot[:, i * q:(i + 1) * q].astype(BF16)
                         else:
-                            y_lc(e, j).start()
+                            dw[y_at(e, j)] = tot
 
         @pl.loop(0, NC)
         def _(j):
@@ -344,24 +349,19 @@
                 for e in range(2):
                     for n in range(3):
                         rc(part.at[me, e, j], recv.at[n, e, j], ss.at[n, e, j], rs.at[n, e, j], {axis: nbr[e]}).wait_send()
+
+        @pl.loop(0, 4)
+        def _(j):
             for e in range(2):
-                @pl.when(j < 4)
-                def _():
-                    for i in range(2):
-                        x_rc(e, j, i).wait()
-                    y_rc(e, j).wait()
-
-                @pl.when(j >= 4)
-                def _():
-                    for i in range(2):
-                        x_lc(e, j, i).wait()
-                    y_lc(e, j).wait()
+                for i in range(2):
+                    x_rc(e, j, i).wait()
+                y_rc(e, j).wait()
 
         for cp in [w_d2d] + g_d2d + x_d2d + w_dir + x_dir + w_fwd + x_fwd:
             cp.wait_send()
 
     pl.run_scoped(reduce, pltpu.VMEM((2, 3, cr, 2 * q), F32), pltpu.VMEM((2, 3, qr, f), F32),
-                  pltpu.VMEM((2, NC, cr, 2 * q), BF16), pltpu.VMEM((2, NC, qr, f), F32))
+                  pltpu.VMEM((2, 4, cr, 2 * q), BF16), pltpu.VMEM((2, 4, qr, f), F32))
 
 
 def solution(mesh):
@@ -376,11 +376,12 @@
         dma = lambda *s: pltpu.SemaphoreType.DMA(s)
         any_ = pl.BlockSpec(memory_space=pl.ANY)
         shapes = [
-            jax.ShapeDtypeStruct((tb, dcols), BF16),
-            jax.ShapeDtypeStruct((wrows, f), F32),
+            pltpu.VMEM((tb, dcols), BF16),
+            pltpu.VMEM((wrows, f), F32),
             jax.ShapeDtypeStruct((4, 2, NC, cr, 2 * q), F32),
             jax.ShapeDtypeStruct((4, 2, NC, qr, f), F32),
             jax.ShapeDtypeStruct((4, 2, 2, tb, q), BF16),
+            jax.ShapeDtypeStruct((4, 2, q, f), BF16),
             jax.ShapeDtypeStruct((3, 2, NC, cr, 2 * q), F32),
             jax.ShapeDtypeStruct((3, 2, NC, qr, f), F32),
         ]
@@ -388,15 +389,14 @@
             kernel,
             out_shape=shapes,
             in_specs=[any_] * 3,
-            out_specs=[any_] * len(shapes),
+            out_specs=[pl.BlockSpec(memory_space=pltpu.VMEM)] * 2 + [any_] * (len(shapes) - 2),
             scratch_shapes=[
                 pltpu.VMEM((2, tb, f), BF16),
-                pltpu.VMEM((4, 2, q, f), BF16),
                 dma(5), dma(7), dma(4), dma(4, 2), dma(4, 2, 2), dma(2, 2), dma(2), dma(2, 2, 2), dma(2, 2),
                 dma(3, 2, NC), dma(3, 2, NC), dma(3, 2, NC), dma(3, 2, NC),
-                dma(2, NC, 2), dma(2, 4, 2), dma(2, NC), dma(2, 4), dma(2, 2), dma(2, 2), dma(2, 2), dma(2, 2, 3),
+                dma(2, 4, 2), dma(2, 4, 2), dma(2, 4), dma(2, 4), dma(2, 2), dma(2, 2), dma(2, 2), dma(2), dma(2, 2, 3),
             ],
-            compiler_params=pltpu.CompilerParams(collective_id=0, has_side_effects=True, vmem_limit_bytes=67043328),
+            compiler_params=pltpu.CompilerParams(collective_id=0, has_side_effects=True, vmem_limit_bytes=52 << 20),
             name="linear_grads",
         )(x, w, g)
         return res[0], res[1]

time: 432 us -> 425 us (0.984)
  local copies, waits for them, and re-layouts: 11.2 us -> 5.06 us
    unnamed x2, local copies, waits for them, and re-layouts: 11.2 us -> 5.06 us
where the time goes in v2:
time: 425 us; the launch traced here: 421 us
  Pallas kernels  415 us (98%)
  local copies, waits for them, and re-layouts  5.06 us (1%)
    pallas_call x1, Pallas kernels, local_step(): pl.pallas_call(kernel, out_shape=shapes, in_specs=[any_] * 3, out_specs=[...  415 us

profile of v2, /device:TPU:104, one launch (start us, length us, event | category | flops | bytes accessed | tf_op | source)
XLA Modules:
  0.0 421.1 jit_solution(890462390818521214)
XLA Ops:
  0.6 415.4 %linear_grads.1 = (bf16[2048,1024]{1,0:T(8,128)(2,1)S(1)}, f32[512,3584]{1,0:T(8,128)S(1)}, f32[4,2,8,256,512]{4,3,2,1,0:T(8,128)}, f32[4,2,8,32,3584]{4,3,2,1,0...) custom-call(bf16[2048,1024]{1,0:T(8,128)(2,1)} %x.1, ...), custom_call_target="tpu_custom_call" | custom-call | tf_op jit(solution)/shard_map/linear_grads/pallas_call | solution.py:388
  416.0 2.0 copy.7
  418.1 3.0 copy.8

commit v3 on v2

v3 whole, which is shorter than its diff:
```python
import functools

import jax
import jax.numpy as jnp
from jax import lax
from jax.experimental import pallas as pl
from jax.experimental.pallas import tpu as pltpu
from jax.sharding import PartitionSpec as P

MESH = pl.DeviceIdType.MESH
BF16, F32 = jnp.bfloat16, jnp.float32
NC = 8
NH = NC // 2


def kernel(x, w, g, dx, dw, pp, qq, xa, wa, rx, ry, gv, vx,
           ls, ss, dr, wr, xr, ring_s, opp_r, pure_r, xacc_r, yacc_r, fin, outs, ads, told):
    h, y, c = lax.axis_index("ro"), lax.axis_index("ri"), lax.axis_index("co")
    o = 1 - h
    tb, dcols = x.shape
    wrows, f = w.shape
    q = wrows // 2
    cr, qr = tb // NC, q // NC
    ft = f // 7
    yn = [lax.rem(y + 1, 4), lax.rem(y + 3, 4)]
    cn = [lax.rem(c + 1, 4), lax.rem(c + 3, 4)]
    y2, c2 = lax.rem(y + 2, 4), lax.rem(c + 2, 4)
    sib = {"ro": o}

    def rc(src, dst, ssem, rsem, dev):
        return pltpu.make_async_remote_copy(src_ref=src, dst_ref=dst, send_sem=ssem, recv_sem=rsem, device_id=dev, device_id_type=MESH)

    def lc(src, dst, sem):
        return pltpu.make_async_copy(src, dst, sem)

    def done(ref, sem):
        lc(ref, ref, sem).wait()

    def xor(a, b):
        return 2 * lax.rem(a // 2 + b // 2, 2) + lax.rem(lax.rem(a, 2) + lax.rem(b, 2), 2)

    bar = pltpu.get_barrier_semaphore()
    partners = [{"co": cn[0], "ro": 0}, {"co": cn[1], "ro": 0}, sib, {"ri": yn[0], "ro": 1}, {"ri": yn[1], "ro": 1}]
    for dev in partners:
        pl.semaphore_signal(bar, 1, device_id=dev, device_id_type=MESH)

    def heard(core):
        @pl.when(h == core)
        def _():
            pl.semaphore_wait(bar, 5)
            pl.semaphore_signal(told, 1, device_id=sib, device_id_type=MESH)

        @pl.when(h != core)
        def _():
            pl.semaphore_wait(told, 1)

    heard(0)

    def xcols(i, k):
        return x.at[:, pl.ds(pl.multiple_of(i * 2 * q + k * q, q), q)]

    def wrow(k):
        return w.at[pl.ds(pl.multiple_of(k * q, q), q)]

    w_dir, x_dir = [], []
    for n in range(2):
        for e in range(2):
            k = h if n == e else o
            w_dir.append(rc(wrow(k), wa.at[y, h], ss.at[3], wr.at[y, h], {"ri": yn[e], "ro": k}))
            for i in range(2):
                x_dir.append(rc(xcols(i, k), xa.at[c, h, i], ss.at[5], xr.at[c, h], {"co": cn[e], "ro": k}))
    w_d2d = rc(wrow(o), wa.at[y, h], ss.at[0], wr.at[y, h], sib)
    g_loc = lc(g, gv.at[h], ls.at[0])
    g_d2d = rc(g, gv.at[h], ss.at[1], dr.at[0], sib)
    x_d2d = [rc(xcols(i, o), xa.at[c, h, i], ss.at[2], xr.at[c, h], sib) for i in range(2)]
    for cp in x_dir + [w_d2d, g_loc, g_d2d] + x_d2d:
        cp.start()
    heard(1)
    for cp in w_dir:
        cp.start()

    w_fwd = [rc(wa.at[yn[1 - e], k], wa.at[yn[1 - e], k], ss.at[4], wr.at[yn[1 - e], k], {"ri": yn[e]}) for e, k in ((0, h), (1, o))]
    x_fwd = [rc(xa.at[cn[1 - e], k], xa.at[cn[1 - e], k], ss.at[6], xr.at[cn[1 - e], k], {"co": cn[e]}) for e, k in ((0, h), (1, o))]

    def got_w(yy, k):
        done(wa.at[yy, k], wr.at[yy, k])

    def got_x(cc, k):
        done(xa.at[cc, k], xr.at[cc, k])

    def sends(a, part, recv, me, axis, nbr, d):
        k = lax.rem(d - me + 4, 4)

        @pl.when(k == 2)
        def _():
            for n in range(2):
                for e in range(2):
                    half = pl.ds(n * NH, NH)
                    rc(part.at[d, e, half], recv.at[0, e, half], ring_s.at[a, 0, e], opp_r.at[a, e, n], {axis: nbr[e]}).start()

        for e in range(2):
            @pl.when(k == 1 + 2 * e)
            def _():
                rc(part.at[d, 1 - e], recv.at[1, e], ring_s.at[a, 1, e], pure_r.at[a, e], {axis: nbr[e]}).start()

    x_sends = functools.partial(sends, 0, pp, rx, c, "co", cn)
    y_sends = functools.partial(sends, 1, qq, ry, y, "ri", yn)

    def compute(wv, xin, xt, pst, qst):
        for i in range(2):
            lc(xcols(i, h), xin.at[0, i], ls.at[2]).start()

        def p_out(slot, r, yy, m):
            s, ab, hf = 1 - m // 4, lax.rem(m // 2, 2), lax.rem(m, 2)
            return lc(pst.at[slot, r], pp.at[2 * r + yy // 2, ab, pl.ds(s * 4 + hf * 2, 2), :, pl.ds(pl.multiple_of(lax.rem(yy, 2) * q, q), q)], outs.at[slot])

        def p_step(yy, first):
            @pl.when(first)
            def _():
                lc(wrow(h), wv.at[pl.ds(pl.multiple_of(h * q, q), q)], ls.at[1]).start()
                lc(wa.at[yy, o], wv.at[pl.ds(pl.multiple_of(o * q, q), q)], ls.at[1]).start()

            @pl.when(jnp.logical_not(first))
            def _():
                for r in range(2):
                    lc(wa.at[yy, r], wv.at[pl.ds(r * q, q)], ls.at[1]).start()

            done(wv, ls.at[1])

            @pl.loop(0, 8)
            def _(m):
                @pl.when(first & (m == 4))
                def _():
                    done(gv.at[o], dr.at[0])

                s, ab, hf = 1 - m // 4, lax.rem(m // 2, 2), lax.rem(m, 2)
                t = s * h + (1 - s) * o
                row = pl.multiple_of(ab * (tb // 2) + hf * (tb // 4), tb // 4)
                slot = lax.rem(m, 2)

                @pl.when(m >= 2)
                def _():
                    done(pst.at[slot], outs.at[slot])

                res = lax.dot_general(gv[t, pl.ds(row, tb // 4), :], wv[...], (((1,), (1,)), ((), ())), preferred_element_type=F32)
                for r in range(2):
                    pst[slot, r] = res[:, r * q:(r + 1) * q].reshape(2, cr, q)
                for r in range(2):
                    p_out(slot, r, yy, m).start()

            for slot in range(2):
                done(pst.at[slot], outs.at[slot])

        def q_out(slot, r, yy, n):
            s = r * h + (1 - r) * o
            return lc(qst.at[slot, r], qq.at[yy, :, pl.ds(s * 4, 4), :, pl.ds(pl.multiple_of(n * ft, ft), ft)], outs.at[slot])

        def q_step(yy):
            for r in range(2):
                for t in range(2):
                    lc(xa.at[2 * r + yy // 2, t, lax.rem(yy, 2)], xin.at[r, t], ls.at[3]).start()
            done(xin, ls.at[3])

            @pl.loop(0, NC)
            def _(n):
                at = pl.ds(pl.multiple_of(n * cr, cr), cr)
                for r in range(2):
                    for t in range(2):
                        xt[t, r * q:(r + 1) * q, at] = xin[r, t, at, :].T

            @pl.loop(0, 7)
            def _(n):
                slot = lax.rem(n, 2)

                @pl.when(n >= 2)
                def _():
                    done(qst.at[slot], outs.at[slot])

                at = pl.ds(pl.multiple_of(n * ft, ft), ft)
                res = jnp.dot(xt[0], gv[0, :, at], preferred_element_type=F32)
                res += jnp.dot(xt[1], gv[1, :, at], preferred_element_type=F32)
                for r in range(2):
                    qst[slot, r] = res[r * q:(r + 1) * q].reshape(2, 4, qr, ft)
                for r in range(2):
                    q_out(slot, r, yy, n).start()

            for slot in range(2):
                done(qst.at[slot], outs.at[slot])

        op = lax.rem(y // 2 + c + 1, 2)
        even = 1 - lax.rem(y, 2)
        rem1 = even * h + (1 - even) * o

        @pl.loop(0, 8)
        def _(step):
            @pl.when(step == 0)
            def _():
                done(gv.at[h], ls.at[0])
                got_w(y, o)

            @pl.when(step == 1)
            def _():
                done(xin.at[0], ls.at[2])
                for i in range(2):
                    lc(xin.at[0, i], xa.at[c, h, i], ls.at[2]).start()
                got_w(yn[1], h)
                w_fwd[0].start()
                got_w(yn[0], o)
                w_fwd[1].start()
                got_x(cn[1], h)
                x_fwd[0].start()
                got_x(cn[0], o)
                x_fwd[1].start()
                got_w(xor(y, 1), rem1)

            @pl.when(step == 2)
            def _():
                x_sends(y // 2)
                x_sends(2 + y // 2)
                got_x(cn[1], o)
                got_x(cn[0], h)
                done(xin.at[0], ls.at[2])

            @pl.when(step == 3)
            def _():
                got_x(c, o)
                got_x(c2, 0)
                got_x(c2, 1)

            @pl.when(step == 5)
            def _():
                got_w(3 - y, 1 - rem1)

            @pl.when(step == 6)
            def _():
                got_w(y2, 0)
                got_w(y2, 1)

            late = step // 5
            is_p = (step < 2) | ((step >= 5) & (step < 7))
            pn = step - 3 * late
            qn = step - 2 - 2 * (step // 7)
            pcode = pn + pn // 2 - 2 * (pn // 3)
            qa = qn // 2
            qcode = op * ((1 - qa) * (2 + qn) + qa * (3 - qn)) + (1 - op) * lax.rem(qn + 1, 4)

            @pl.when(is_p)
            def _():
                p_step(xor(y, pcode), step == 0)

            @pl.when(jnp.logical_not(is_p))
            def _():
                yy = xor(y, qcode)
                q_step(yy)
                y_sends(yy)

            @pl.when(step == 6)
            def _():
                x_sends(1 - y // 2)
                x_sends(3 - y // 2)

    pl.run_scoped(compute, pltpu.VMEM((2 * q, f), BF16), pltpu.VMEM((2, 2, tb, q), BF16), pltpu.VMEM((2, 2 * q, tb), BF16),
                  pltpu.VMEM((2, 2, 2, cr, q), F32), pltpu.VMEM((2, 2, 2, 4, qr, ft), F32))

    def reduce(ax, ay, bx, by, px):
        rings = ((0, pp, rx, c, cn, "co", ax), (1, qq, ry, y, yn, "ri", ay))

        @pl.loop(0, 2)
        def _(n):
            for a, part, recv, me, nbr, axis, buf in rings:
                for e in range(2):
                    done(recv.at[0, e, pl.ds(0, NH)], opp_r.at[a, e, n])

            @pl.loop(0, NH)
            def _(i):
                j = n * NH + i
                for a, part, recv, me, nbr, axis, buf in rings:
                    for e in range(2):
                        lc(part.at[nbr[e], e, j], buf.at[e, 0], ads.at[a, 0]).start()
                        lc(recv.at[0, e, j], buf.at[e, 1], ads.at[a, 0]).start()
                for a, part, recv, me, nbr, axis, buf in rings:
                    done(buf.at[:, pl.ds(0, 2)], ads.at[a, 0])
                    for e in range(2):
                        buf[e, 2] = buf[e, 0] + buf[e, 1]
                        lc(buf.at[e, 2], part.at[nbr[e], e, j], ads.at[a, 1]).start()
                for a, part, recv, me, nbr, axis, buf in rings:
                    done(buf.at[:, 2], ads.at[a, 1])

                @pl.when(n == 1)
                def _():
                    for e in range(2):
                        rc(pp.at[cn[e], e, j], vx.at[e, i], ring_s.at[0, 2, e], xacc_r.at[e, 1 + i], {"co": cn[e]}).start()

            half = pl.ds(n * NH, NH)

            @pl.when(n == 0)
            def _():
                for e in range(2):
                    rc(pp.at[cn[e], e, half], rx.at[2, e, half], ring_s.at[0, 2, e], xacc_r.at[e, 0], {"co": cn[e]}).start()

            for e in range(2):
                rc(qq.at[yn[e], e, half], ry.at[2, e, half], ring_s.at[1, 2, e], yacc_r.at[e, n], {"ri": yn[e]}).start()

        def x_at(e, j, i):
            return (pl.ds(pl.multiple_of(e * (tb // 2) + j * cr, cr), cr), pl.ds(pl.multiple_of(i * 2 * q + h * q, q), q))

        def y_at(e, j):
            return pl.ds(pl.multiple_of(h * q + e * (q // 2) + j * qr, qr), qr)

        def load(ring, j, third):
            a, part, recv, me, nbr, axis, buf = ring
            for e in range(2):
                lc(part.at[me, e, j], buf.at[e, 0], ads.at[a, 0]).start()
                lc(recv.at[1, 1 - e, j], buf.at[e, 1], ads.at[a, 0]).start()
                if third:
                    lc(recv.at[2, e, j], buf.at[e, 2], ads.at[a, 0]).start()
            done(buf if third else buf.at[:, pl.ds(0, 2)], ads.at[a, 0])

        for a, part, recv, me, nbr, axis, buf in rings:
            for e in range(2):
                done(recv.at[1, e], pure_r.at[a, e])
                done(part.at[0, e], ring_s.at[a, 0, e])
                done(part.at[0, e], ring_s.at[a, 1, e])
        done(wa.at[0, 0], ss.at[0])
        done(gv.at[0], ss.at[1])
        done(xa.at[0, 0], ss.at[2])
        done(wa.at[pl.ds(0, 2)], ss.at[3])
        done(wa.at[0], ss.at[4])
        done(xa.at[pl.ds(0, 2)], ss.at[5])
        done(xa.at[0], ss.at[6])

        for e in range(2):
            done(ry.at[2, e, pl.ds(0, NH)], yacc_r.at[e, 0])

        @pl.loop(0, NH)
        def _(j):
            load(rings[1], j, True)
            for e in range(2):
                by[e, j] = ay[e, 0] + ay[e, 1] + ay[e, 2]
                rc(by.at[e, j], dw.at[y_at(e, j)], fin.at[2], fin.at[3], sib).start()
            load(rings[1], NH + j, False)
            for e in range(2):
                dw[y_at(e, j)] = ay[e, 0] + ay[e, 1]

        for e in range(2):
            done(rx.at[2, e, pl.ds(0, NH)], xacc_r.at[e, 0])

        @pl.loop(0, NH)
        def _(j):
            load(rings[0], j, True)
            for e in range(2):
                bx[e, j] = (ax[e, 0] + ax[e, 1] + ax[e, 2]).astype(BF16)
                for i in range(2):
                    rc(bx.at[e, j, :, i * q:(i + 1) * q], dx.at[x_at(e, j, i)], fin.at[0], fin.at[1], sib).start()
            load(rings[0], NH + j, False)
            for e in range(2):
                px[e, j] = ax[e, 0] + ax[e, 1]

        for e in range(2):
            done(ry.at[2, e, pl.ds(0, NH)], yacc_r.at[e, 1])

        @pl.loop(0, NH)
        def _(j):
            for e in range(2):
                lc(ry.at[2, e, NH + j], ay.at[e, 2], ads.at[1, 0]).start()
            done(ay.at[:, 2], ads.at[1, 0])
            for e in range(2):
                dw[y_at(e, j)] += ay[e, 2]

        for n in range(4):
            done(by if n >= 2 else bx, fin.at[n])
        for e in range(2):
            done(qq.at[0, e], ring_s.at[1, 2, e])

        @pl.loop(0, NH)
        def _(j):
            for e in range(2):
                done(vx.at[e, j], xacc_r.at[e, 1 + j])
                tot = px[e, j] + vx[e, j]
                for i in range(2):
                    dx[x_at(e, j, i)] = tot[:, i * q:(i + 1) * q].astype(BF16)

        for e in range(2):
            done(pp.at[0, e], ring_s.at[0, 2, e])

    pl.run_scoped(reduce, pltpu.VMEM((2, 3, cr, 2 * q), F32), pltpu.VMEM((2, 3, qr, f), F32),
                  pltpu.VMEM((2, NH, cr, 2 * q), BF16), pltpu.VMEM((2, NH, qr, f), F32), pltpu.VMEM((2, NH, cr, 2 * q), F32))


def put_kernel(a, b, u, v, sems):
    for i, (src, dst) in enumerate(((b, v), (a, u))):
        rows = src.shape[0] // 4
        for n in range(4):
            pltpu.make_async_copy(src.at[pl.ds(n * rows, rows)], dst.at[pl.ds(n * rows, rows)], sems.at[i]).start()
    for i, (src, dst) in enumerate(((b, v), (a, u))):
        pltpu.make_async_copy(src, dst, sems.at[i]).wait()


def solution(mesh):
    spec_act = P(("dp", "ro", "ri"), "co")
    spec_w = P(("ro", "ri"), "co")

    def local_step(x, w, g):
        tb, dcols = x.shape
        wrows, f = w.shape
        q = wrows // 2
        cr, qr = tb // NC, q // NC
        dma = lambda *s: pltpu.SemaphoreType.DMA(s)
        any_ = pl.BlockSpec(memory_space=pl.ANY)
        vmem = pl.BlockSpec(memory_space=pltpu.VMEM)
        shapes = [
            pltpu.VMEM((tb, dcols), BF16),
            pltpu.VMEM((wrows, f), F32),
            jax.ShapeDtypeStruct((4, 2, NC, cr, 2 * q), F32),
            jax.ShapeDtypeStruct((4, 2, NC, qr, f), F32),
            jax.ShapeDtypeStruct((4, 2, 2, tb, q), BF16),
            jax.ShapeDtypeStruct((4, 2, q, f), BF16),
            jax.ShapeDtypeStruct((3, 2, NC, cr, 2 * q), F32),
            jax.ShapeDtypeStruct((3, 2, NC, qr, f), F32),
        ]
        res = pl.pallas_call(
            kernel,
            out_shape=shapes,
            in_specs=[any_] * 3,
            out_specs=[vmem] * 2 + [any_] * (len(shapes) - 2),
            scratch_shapes=[
                pltpu.VMEM((2, tb, f), BF16),
                pltpu.VMEM((2, NH, cr, 2 * q), F32),
                dma(4), dma(7), dma(1), dma(4, 2), dma(4, 2), dma(2, 3, 2), dma(2, 2, 2), dma(2, 2), dma(2, 1 + NH), dma(2, 2), dma(4), dma(2), dma(2, 2), pltpu.SemaphoreType.REGULAR,
            ],
            compiler_params=pltpu.CompilerParams(collective_id=0, has_side_effects=True, vmem_limit_bytes=52 << 20),
            name="linear_grads",
        )(x, w, g)
        return pl.pallas_call(
            put_kernel,
            out_shape=[jax.ShapeDtypeStruct(r.shape, r.dtype) for r in res[:2]],
            in_specs=[vmem] * 2,
            out_specs=[any_] * 2,
            scratch_shapes=[dma(2)],
            compiler_params=pltpu.CompilerParams(vmem_limit_bytes=16 << 20),
            name="put",
        )(res[0], res[1])

    return jax.shard_map(local_step, mesh=mesh, in_specs=(spec_act, spec_w, spec_act), out_specs=(spec_act, spec_act), check_vma=False)
```

time: 425 us -> 417 us (0.981)
  local copies, waits for them, and re-layouts: 5.06 us -> 0 us
    unnamed x2 -> x0, local copies, waits for them, and re-layouts: 5.06 us -> none
    pallas_call x1, Pallas kernels: 415 us -> 411 us  [local_step(): pl.pallas_call(kernel, out_shape=shapes, in_specs=[any_] * 3, out_specs=[...]
    pallas_call x0 -> x1, Pallas kernels: none -> 4.3 us  [local_step(): pl.pallas_call(put_kernel, out_shape=[jax.ShapeDtypeStruct(r.shape, r.dty...]
where the time goes in v3:
time: 417 us; the launch traced here: 415 us
  Pallas kernels  415 us (100%)
    pallas_call x1, Pallas kernels, local_step(): pl.pallas_call(kernel, out_shape=shapes, in_specs=[any_] * 3, out_specs=[...  411 us

profile of v3, /device:TPU:104, one launch (start us, length us, event | category | flops | bytes accessed | tf_op | source)
XLA Modules:
  0.0 415.5 jit_solution(15512627914626935033)
XLA Ops:
  0.6 410.6 %linear_grads.1 = (bf16[2048,1024]{1,0:T(8,128)(2,1)S(1)}, f32[512,3584]{1,0:T(8,128)S(1)}, f32[4,2,8,256,512]{4,3,2,1,0:T(8,128)}, f32[4,2,8,32,3584]{4,3,2,1,0...) custom-call(bf16[2048,1024]{1,0:T(8,128)(2,1)} %x.1, ...), custom_call_target="tpu_custom_call" | custom-call | tf_op jit(solution)/shard_map/linear_grads/pallas_call | solution.py:421
  411.2 4.3 %put.1 = (bf16[2048,1024]{1,0:T(8,128)(2,1)}, f32[512,3584]{1,0:T(8,128)}) custom-call(bf16[2048,1024]{1,0:T(8,128)(2,1)S(1)} %get-tuple-element.4.a, f32[512,3584]{1,0:T(8,128)S(1)} %get-tuple-element.5.b), custom_call_target="tpu_custom_call" | custom-call | tf_op jit(solution)/shard_map/put/pallas_call | solution.py:434

commit v4 on v0

v4 whole, which is shorter than its diff:
```python
import functools

import jax
import jax.numpy as jnp
from jax import lax
from jax.experimental import pallas as pl
from jax.experimental.pallas import tpu as pltpu
from jax.sharding import PartitionSpec as P

MESH = pl.DeviceIdType.MESH
BF16, F32 = jnp.bfloat16, jnp.float32
NC = 8
NH = NC // 2


def kernel(x, w, g, dx, dw, pp, qq, xa, wa, rx, ry, gv, vx,
           ss, dr, wr, xr, opp_r, pure_r, xacc_r, yacc_r, fin_r, told):
    h, y, c = lax.axis_index("ro"), lax.axis_index("ri"), lax.axis_index("co")
    o = 1 - h
    tb, dcols = x.shape
    wrows, f = w.shape
    q = wrows // 2
    cr, qr = tb // NC, q // NC
    ft = f // 7
    yn = [lax.rem(y + 1, 4), lax.rem(y + 3, 4)]
    cn = [lax.rem(c + 1, 4), lax.rem(c + 3, 4)]
    y2, c2 = lax.rem(y + 2, 4), lax.rem(c + 2, 4)
    sib = {"ro": o}

    def rc(src, dst, ssem, rsem, dev):
        return pltpu.make_async_remote_copy(src_ref=src, dst_ref=dst, send_sem=ssem, recv_sem=rsem, device_id=dev, device_id_type=MESH)

    def lc(src, dst, sem):
        return pltpu.make_async_copy(src, dst, sem)

    def done(ref, sem):
        lc(ref, ref, sem).wait()

    def xor(a, b):
        return 2 * lax.rem(a // 2 + b // 2, 2) + lax.rem(lax.rem(a, 2) + lax.rem(b, 2), 2)

    bar = pltpu.get_barrier_semaphore()
    partners = [{"co": cn[0], "ro": 0}, {"co": cn[1], "ro": 0}, sib, {"ri": yn[0], "ro": 1}, {"ri": yn[1], "ro": 1}]
    for dev in partners:
        pl.semaphore_signal(bar, 1, device_id=dev, device_id_type=MESH)

    def heard(core):
        @pl.when(h == core)
        def _():
            pl.semaphore_wait(bar, 5)
            pl.semaphore_signal(told, 1, device_id=sib, device_id_type=MESH)

        @pl.when(h != core)
        def _():
            pl.semaphore_wait(told, 1)

    heard(0)

    def xcols(i, k):
        return x.at[:, pl.ds(pl.multiple_of(i * 2 * q + k * q, q), q)]

    def wrow(k):
        return w.at[pl.ds(pl.multiple_of(k * q, q), q)]

    w_dir, x_dir = [], []
    for n in range(2):
        for e in range(2):
            k = h if n == e else o
            w_dir.append(rc(wrow(k), wa.at[y, h], ss.at[0], wr.at[y, h], {"ri": yn[e], "ro": k}))
            for i in range(2):
                x_dir.append(rc(xcols(i, k), xa.at[c, h, i], ss.at[1], xr.at[c, h], {"co": cn[e], "ro": k}))
    for cp in x_dir:
        cp.start()

    def rest(ring_s, fin, ls, outs, ads):
        w_d2d = rc(wrow(o), wa.at[y, h], ss.at[2], wr.at[y, h], sib)
        g_loc = lc(g, gv.at[h], ls.at[0])
        g_d2d = rc(g, gv.at[h], ss.at[3], dr.at[0], sib)
        x_d2d = [rc(xcols(i, o), xa.at[c, h, i], ss.at[4], xr.at[c, h], sib) for i in range(2)]
        for cp in [w_d2d, g_loc, g_d2d] + x_d2d:
            cp.start()
        heard(1)
        for cp in w_dir:
            cp.start()

        w_fwd = [rc(wa.at[yn[1 - e], k], wa.at[yn[1 - e], k], ss.at[0], wr.at[yn[1 - e], k], {"ri": yn[e]}) for e, k in ((0, h), (1, o))]
        x_fwd = [rc(xa.at[cn[1 - e], k], xa.at[cn[1 - e], k], ss.at[1], xr.at[cn[1 - e], k], {"co": cn[e]}) for e, k in ((0, h), (1, o))]

        def got_w(yy, k):
            done(wa.at[yy, k], wr.at[yy, k])

        def got_x(cc, k):
            done(xa.at[cc, k], xr.at[cc, k])

        def sends(a, part, recv, me, axis, nbr, d):
            k = lax.rem(d - me + 4, 4)

            @pl.when(k == 2)
            def _():
                for n in range(2):
                    for e in range(2):
                        half = pl.ds(n * NH, NH)
                        rc(part.at[d, e, half], recv.at[0, e, half], ring_s.at[a], opp_r.at[a, e, n], {axis: nbr[e]}).start()

            for e in range(2):
                @pl.when(k == 1 + 2 * e)
                def _():
                    rc(part.at[d, 1 - e], recv.at[1, e], ring_s.at[a], pure_r.at[a, e], {axis: nbr[e]}).start()

        x_sends = functools.partial(sends, 0, pp, rx, c, "co", cn)
        y_sends = functools.partial(sends, 1, qq, ry, y, "ri", yn)

        def compute(wv, xin, xt, pst, qst):
            for i in range(2):
                lc(xcols(i, h), xin.at[0, i], ls.at[2]).start()

            def p_out(slot, r, yy, m):
                s, ab, hf = 1 - m // 4, lax.rem(m // 2, 2), lax.rem(m, 2)
                return lc(pst.at[slot, r], pp.at[2 * r + yy // 2, ab, pl.ds(s * 4 + hf * 2, 2), :, pl.ds(pl.multiple_of(lax.rem(yy, 2) * q, q), q)], outs.at[slot])

            def p_step(yy, first):
                @pl.when(first)
                def _():
                    lc(wrow(h), wv.at[pl.ds(pl.multiple_of(h * q, q), q)], ls.at[1]).start()
                    lc(wa.at[yy, o], wv.at[pl.ds(pl.multiple_of(o * q, q), q)], ls.at[1]).start()

                @pl.when(jnp.logical_not(first))
                def _():
                    for r in range(2):
                        lc(wa.at[yy, r], wv.at[pl.ds(r * q, q)], ls.at[1]).start()

                done(wv, ls.at[1])

                @pl.loop(0, 8)
                def _(m):
                    @pl.when(first & (m == 4))
                    def _():
                        done(gv.at[o], dr.at[0])

                    s, ab, hf = 1 - m // 4, lax.rem(m // 2, 2), lax.rem(m, 2)
                    t = s * h + (1 - s) * o
                    row = pl.multiple_of(ab * (tb // 2) + hf * (tb // 4), tb // 4)
                    slot = lax.rem(m, 2)

                    @pl.when(m >= 2)
                    def _():
                        done(pst.at[slot], outs.at[slot])

                    res = lax.dot_general(gv[t, pl.ds(row, tb // 4), :], wv[...], (((1,), (1,)), ((), ())), preferred_element_type=F32)
                    for r in range(2):
                        pst[slot, r] = res[:, r * q:(r + 1) * q].reshape(2, cr, q)
                    for r in range(2):
                        p_out(slot, r, yy, m).start()

                for slot in range(2):
                    done(pst.at[slot], outs.at[slot])

            def q_out(slot, r, yy, n):
                s = r * h + (1 - r) * o
                return lc(qst.at[slot, r], qq.at[yy, :, pl.ds(s * 4, 4), :, pl.ds(pl.multiple_of(n * ft, ft), ft)], outs.at[slot])

            def q_step(yy):
                for r in range(2):
                    for t in range(2):
                        lc(xa.at[2 * r + yy // 2, t, lax.rem(yy, 2)], xin.at[r, t], ls.at[3]).start()
                done(xin, ls.at[3])

                @pl.loop(0, NC)
                def _(n):
                    at = pl.ds(pl.multiple_of(n * cr, cr), cr)
                    for r in range(2):
                        for t in range(2):
                            xt[t, r * q:(r + 1) * q, at] = xin[r, t, at, :].T

                @pl.loop(0, 7)
                def _(n):
                    slot = lax.rem(n, 2)

                    @pl.when(n >= 2)
                    def _():
                        done(qst.at[slot], outs.at[slot])

                    at = pl.ds(pl.multiple_of(n * ft, ft), ft)
                    res = jnp.dot(xt[0], gv[0, :, at], preferred_element_type=F32)
                    res += jnp.dot(xt[1], gv[1, :, at], preferred_element_type=F32)
                    for r in range(2):
                        qst[slot, r] = res[r * q:(r + 1) * q].reshape(2, 4, qr, ft)
                    for r in range(2):
                        q_out(slot, r, yy, n).start()

                for slot in range(2):
                    done(qst.at[slot], outs.at[slot])

            op = lax.rem(y // 2 + c + 1, 2)
            even = 1 - lax.rem(y, 2)
            rem1 = even * h + (1 - even) * o

            @pl.loop(0, 8)
            def _(step):
                @pl.when(step == 0)
                def _():
                    done(gv.at[h], ls.at[0])
                    got_w(y, o)

                @pl.when(step == 1)
                def _():
                    done(xin.at[0], ls.at[2])
                    for i in range(2):
                        lc(xin.at[0, i], xa.at[c, h, i], ls.at[2]).start()
                    got_w(yn[1], h)
                    w_fwd[0].start()
                    got_w(yn[0], o)
                    w_fwd[1].start()
                    got_x(cn[1], h)
                    x_fwd[0].start()
                    got_x(cn[0], o)
                    x_fwd[1].start()
                    got_w(xor(y, 1), rem1)

                @pl.when(step == 2)
                def _():
                    x_sends(y // 2)
                    x_sends(2 + y // 2)
                    got_x(cn[1], o)
                    got_x(cn[0], h)
                    done(xin.at[0], ls.at[2])

                @pl.when(step == 3)
                def _():
                    got_x(c, o)
                    got_x(c2, 0)
                    got_x(c2, 1)

                @pl.when(step == 5)
                def _():
                    got_w(3 - y, 1 - rem1)

                @pl.when(step == 6)
                def _():
                    got_w(y2, 0)
                    got_w(y2, 1)

                late = step // 5
                is_p = (step < 2) | ((step >= 5) & (step < 7))
                pn = step - 3 * late
                qn = step - 2 - 2 * (step // 7)
                pcode = pn + pn // 2 - 2 * (pn // 3)
                qa = qn // 2
                qcode = op * ((1 - qa) * (2 + qn) + qa * (3 - qn)) + (1 - op) * lax.rem(qn + 1, 4)

                @pl.when(is_p)
                def _():
                    p_step(xor(y, pcode), step == 0)

                @pl.when(jnp.logical_not(is_p))
                def _():
                    yy = xor(y, qcode)
                    q_step(yy)
                    y_sends(yy)

                @pl.when(step == 6)
                def _():
                    x_sends(1 - y // 2)
                    x_sends(3 - y // 2)

        pl.run_scoped(compute, pltpu.VMEM((2 * q, f), BF16), pltpu.VMEM((2, 2, tb, q), BF16), pltpu.VMEM((2, 2 * q, tb), BF16),
                      pltpu.VMEM((2, 2, 2, cr, q), F32), pltpu.VMEM((2, 2, 2, 4, qr, ft), F32))

        def reduce(ax, ay, bx, by, px):
            rings = ((0, pp, rx, c, cn, "co", ax), (1, qq, ry, y, yn, "ri", ay))

            @pl.loop(0, 2)
            def _(n):
                for a, part, recv, me, nbr, axis, buf in rings:
                    for e in range(2):
                        done(recv.at[0, e, pl.ds(0, NH)], opp_r.at[a, e, n])

                @pl.loop(0, NH)
                def _(i):
                    j = n * NH + i
                    for a, part, recv, me, nbr, axis, buf in rings:
                        for e in range(2):
                            lc(part.at[nbr[e], e, j], buf.at[e, 0], ads.at[a, 0]).start()
                            lc(recv.at[0, e, j], buf.at[e, 1], ads.at[a, 0]).start()
                    for a, part, recv, me, nbr, axis, buf in rings:
                        done(buf.at[:, pl.ds(0, 2)], ads.at[a, 0])
                        for e in range(2):
                            buf[e, 2] = buf[e, 0] + buf[e, 1]
                            lc(buf.at[e, 2], part.at[nbr[e], e, j], ads.at[a, 1]).start()
                    for a, part, recv, me, nbr, axis, buf in rings:
                        done(buf.at[:, 2], ads.at[a, 1])

                    @pl.when(n == 1)
                    def _():
                        for e in range(2):
                            rc(pp.at[cn[e], e, j], vx.at[e, i], ring_s.at[0], xacc_r.at[e, 1 + i], {"co": cn[e]}).start()

                half = pl.ds(n * NH, NH)

                @pl.when(n == 0)
                def _():
                    for e in range(2):
                        rc(pp.at[cn[e], e, half], rx.at[2, e, half], ring_s.at[0], xacc_r.at[e, 0], {"co": cn[e]}).start()

                for e in range(2):
                    rc(qq.at[yn[e], e, half], ry.at[2, e, half], ring_s.at[1], yacc_r.at[e, n], {"ri": yn[e]}).start()

            def x_at(e, j, i):
                return (pl.ds(pl.multiple_of(e * (tb // 2) + j * cr, cr), cr), pl.ds(pl.multiple_of(i * 2 * q + h * q, q), q))

            def y_at(e, j):
                return pl.ds(pl.multiple_of(h * q + e * (q // 2) + j * qr, qr), qr)

            def load(ring, j, third):
                a, part, recv, me, nbr, axis, buf = ring
                for e in range(2):
                    lc(part.at[me, e, j], buf.at[e, 0], ads.at[a, 0]).start()
                    lc(recv.at[1, 1 - e, j], buf.at[e, 1], ads.at[a, 0]).start()
                    if third:
                        lc(recv.at[2, e, j], buf.at[e, 2], ads.at[a, 0]).start()
                done(buf if third else buf.at[:, pl.ds(0, 2)], ads.at[a, 0])

            for a, part, recv, me, nbr, axis, buf in rings:
                for e in range(2):
                    done(recv.at[1, e], pure_r.at[a, e])
            done(wa.at[pl.ds(0, 3)], ss.at[0])
            done(xa.at[pl.ds(0, 3)], ss.at[1])
            done(wa.at[0, 0], ss.at[2])
            done(gv.at[0], ss.at[3])
            done(xa.at[0, 0], ss.at[4])

            for e in range(2):
                done(ry.at[2, e, pl.ds(0, NH)], yacc_r.at[e, 0])

            @pl.loop(0, NH)
            def _(j):
                load(rings[1], j, True)
                for e in range(2):
                    by[e, j] = ay[e, 0] + ay[e, 1] + ay[e, 2]
                    rc(by.at[e, j], dw.at[y_at(e, j)], fin.at[1], fin_r.at[1], sib).start()
                load(rings[1], NH + j, False)
                for e in range(2):
                    dw[y_at(e, j)] = ay[e, 0] + ay[e, 1]

            for e in range(2):
                done(rx.at[2, e, pl.ds(0, NH)], xacc_r.at[e, 0])

            @pl.loop(0, NH)
            def _(j):
                load(rings[0], j, True)
                for e in range(2):
                    bx[e, j] = (ax[e, 0] + ax[e, 1] + ax[e, 2]).astype(BF16)
                    for i in range(2):
                        rc(bx.at[e, j, :, i * q:(i + 1) * q], dx.at[x_at(e, j, i)], fin.at[0], fin_r.at[0], sib).start()
                load(rings[0], NH + j, False)
                for e in range(2):
                    px[e, j] = ax[e, 0] + ax[e, 1]

            for e in range(2):
                done(ry.at[2, e, pl.ds(0, NH)], yacc_r.at[e, 1])

            @pl.loop(0, NH)
            def _(j):
                for e in range(2):
                    lc(ry.at[2, e, NH + j], ay.at[e, 2], ads.at[1, 0]).start()
                done(ay.at[:, 2], ads.at[1, 0])
                for e in range(2):
                    dw[y_at(e, j)] += ay[e, 2]

            for n, ref in enumerate((bx, by)):
                done(ref, fin.at[n])
                done(ref, fin_r.at[n])
            done(ry, ring_s.at[1])

            @pl.loop(0, NH)
            def _(j):
                for e in range(2):
                    done(vx.at[e, j], xacc_r.at[e, 1 + j])
                    tot = px[e, j] + vx[e, j]
                    for i in range(2):
                        dx[x_at(e, j, i)] = tot[:, i * q:(i + 1) * q].astype(BF16)

            done(rx, ring_s.at[0])

        pl.run_scoped(reduce, pltpu.VMEM((2, 3, cr, 2 * q), F32), pltpu.VMEM((2, 3, qr, f), F32),
                      pltpu.VMEM((2, NH, cr, 2 * q), BF16), pltpu.VMEM((2, NH, qr, f), F32), pltpu.VMEM((2, NH, cr, 2 * q), F32))

    dma = pltpu.SemaphoreType.DMA
    pl.run_scoped(rest, dma((2,)), dma((2,)), dma((4,)), dma((2,)), dma((2, 2)))


def put_kernel(a, b, u, v, sems):
    for i, (src, dst) in enumerate(((b, v), (a, u))):
        rows = src.shape[0] // 4
        for n in range(4):
            pltpu.make_async_copy(src.at[pl.ds(n * rows, rows)], dst.at[pl.ds(n * rows, rows)], sems.at[i]).start()
    for i, (src, dst) in enumerate(((b, v), (a, u))):
        pltpu.make_async_copy(src, dst, sems.at[i]).wait()


def solution(mesh):
    spec_act = P(("dp", "ro", "ri"), "co")
    spec_w = P(("ro", "ri"), "co")

    def local_step(x, w, g):
        tb, dcols = x.shape
        wrows, f = w.shape
        q = wrows // 2
        cr, qr = tb // NC, q // NC
        dma = lambda *s: pltpu.SemaphoreType.DMA(s)
        any_ = pl.BlockSpec(memory_space=pl.ANY)
        vmem = pl.BlockSpec(memory_space=pltpu.VMEM)
        shapes = [
            pltpu.VMEM((tb, dcols), BF16),
            pltpu.VMEM((wrows, f), F32),
            jax.ShapeDtypeStruct((4, 2, NC, cr, 2 * q), F32),
            jax.ShapeDtypeStruct((4, 2, NC, qr, f), F32),
            jax.ShapeDtypeStruct((4, 2, 2, tb, q), BF16),
            jax.ShapeDtypeStruct((4, 2, q, f), BF16),
            jax.ShapeDtypeStruct((3, 2, NC, cr, 2 * q), F32),
            jax.ShapeDtypeStruct((3, 2, NC, qr, f), F32),
        ]
        res = pl.pallas_call(
            kernel,
            out_shape=shapes,
            in_specs=[any_] * 3,
            out_specs=[vmem] * 2 + [any_] * (len(shapes) - 2),
            scratch_shapes=[
                pltpu.VMEM((2, tb, f), BF16),
                pltpu.VMEM((2, NH, cr, 2 * q), F32),
                dma(5), dma(1), dma(4, 2), dma(4, 2), dma(2, 2, 2), dma(2, 2), dma(2, 1 + NH), dma(2, 2), dma(2), pltpu.SemaphoreType.REGULAR,
            ],
            compiler_params=pltpu.CompilerParams(collective_id=0, has_side_effects=True, vmem_limit_bytes=52 << 20),
            name="linear_grads",
        )(x, w, g)
        return pl.pallas_call(
            put_kernel,
            out_shape=[jax.ShapeDtypeStruct(r.shape, r.dtype) for r in res[:2]],
            in_specs=[vmem] * 2,
            out_specs=[any_] * 2,
            scratch_shapes=[dma(2)],
            compiler_params=pltpu.CompilerParams(vmem_limit_bytes=16 << 20),
            name="put",
        )(res[0], res[1])

    return jax.shard_map(local_step, mesh=mesh, in_specs=(spec_act, spec_w, spec_act), out_specs=(spec_act, spec_act), check_vma=False)
```

time: 1160 us -> 417 us (0.36)
  waiting for transfers between devices: 994 us -> 0 us
  Pallas kernels: 0 us -> 415 us
  matrix products: 142 us -> 0 us
  between operations: 13.8 us -> 0.64 us
    reduce_scatter x2 -> x0, waiting for transfers between devices: 769 us -> none  [the longest x1 557 us: local_step(): lax.psum_scatter(gw_part, row_axes, scatter_dimension=0, tiled=True)]
    pallas_call x0 -> x2, Pallas kernels: none -> 415 us  [the longest x1 410 us: local_step(): pl.pallas_call(kernel, out_shape=shapes, in_specs=[any_] * 3, out_specs=[...]
    all_gather x2 -> x0, waiting for transfers between devices: 223 us -> none  [the longest x1 140 us: local_step(): w_cols = lax.all_gather(w_blk, row_axes, axis=0, tiled=True)]
    dot_general x2 -> x0, matrix products: 142 us -> none  [the longest x1 71 us: local_step(): lax.dot_general(g_blk, w_cols, (((1,), (1,)), ((), ())), preferred_elemen...]
  transfers between devices with their start and end apart: 4 -> 0, of which waited for: 4 -> 0; matrix products, arithmetic and copies ran while one was open for 13% -> 0% of each run, Pallas kernels for 0% -> 0%
where the time goes in v4:
time: 417 us; the launch traced here: 415 us
  Pallas kernels  415 us (100%)
    pallas_call x1, Pallas kernels, local_step(): pl.pallas_call(kernel, out_shape=shapes, in_specs=[any_] * 3, out_specs=[...  410 us

profile of v4, /device:TPU:104, one launch (start us, length us, event | category | flops | bytes accessed | tf_op | source)
XLA Modules:
  0.0 415.3 jit_solution(8880708040843362972)
XLA Ops:
  0.6 410.3 %linear_grads.1 = (bf16[2048,1024]{1,0:T(8,128)(2,1)S(1)}, f32[512,3584]{1,0:T(8,128)S(1)}, f32[4,2,8,256,512]{4,3,2,1,0:T(8,128)}, f32[4,2,8,32,3584]{4,3,2,1,0...) custom-call(bf16[2048,1024]{1,0:T(8,128)(2,1)} %x.1, ...), custom_call_target="tpu_custom_call" | custom-call | tf_op jit(solution)/shard_map/linear_grads/pallas_call | solution.py:423
  411.0 4.3 %put.1 = (bf16[2048,1024]{1,0:T(8,128)(2,1)}, f32[512,3584]{1,0:T(8,128)}) custom-call(bf16[2048,1024]{1,0:T(8,128)(2,1)S(1)} %get-tuple-element.4.a, f32[512,3584]{1,0:T(8,128)S(1)} %get-tuple-element.5.b), custom_call_target="tpu_custom_call" | custom-call | tf_op jit(solution)/shard_map/put/pallas_call | solution.py:436

commit v5 on v4

--- a/solution.py
+++ b/solution.py
@@ -40,21 +40,20 @@
         return 2 * lax.rem(a // 2 + b // 2, 2) + lax.rem(lax.rem(a, 2) + lax.rem(b, 2), 2)
 
     bar = pltpu.get_barrier_semaphore()
-    partners = [{"co": cn[0], "ro": 0}, {"co": cn[1], "ro": 0}, sib, {"ri": yn[0], "ro": 1}, {"ri": yn[1], "ro": 1}]
-    for dev in partners:
-        pl.semaphore_signal(bar, 1, device_id=dev, device_id_type=MESH)
-
-    def heard(core):
-        @pl.when(h == core)
-        def _():
-            pl.semaphore_wait(bar, 5)
-            pl.semaphore_signal(told, 1, device_id=sib, device_id_type=MESH)
-
-        @pl.when(h != core)
-        def _():
-            pl.semaphore_wait(told, 1)
-
-    heard(0)
+    for e in range(2):
+        pl.semaphore_signal(bar, 1, device_id={"co": cn[e]}, device_id_type=MESH)
+    for e in range(2):
+        pl.semaphore_signal(bar, 1, device_id={"ri": yn[e], "ro": 0}, device_id_type=MESH)
+
+    @pl.when(h == 1)
+    def _():
+        pl.semaphore_signal(bar, 1, device_id=sib, device_id_type=MESH)
+        pl.semaphore_wait(bar, 2)
+
+    @pl.when(h == 0)
+    def _():
+        pl.semaphore_wait(bar, 7)
+        pl.semaphore_signal(told, 1, device_id=sib, device_id_type=MESH)
 
     def xcols(i, k):
         return x.at[:, pl.ds(pl.multiple_of(i * 2 * q + k * q, q), q)]
@@ -62,35 +61,43 @@
     def wrow(k):
         return w.at[pl.ds(pl.multiple_of(k * q, q), q)]
 
-    w_dir, x_dir = [], []
+    def x_send(e, k, i):
+        return rc(xcols(i, k), xa.at[c, h, i], ss.at[1], xr.at[c, h, i], {"co": cn[e], "ro": k})
+
     for n in range(2):
         for e in range(2):
-            k = h if n == e else o
-            w_dir.append(rc(wrow(k), wa.at[y, h], ss.at[0], wr.at[y, h], {"ri": yn[e], "ro": k}))
-            for i in range(2):
-                x_dir.append(rc(xcols(i, k), xa.at[c, h, i], ss.at[1], xr.at[c, h], {"co": cn[e], "ro": k}))
-    for cp in x_dir:
-        cp.start()
+            x_send(e, h, n if e == 0 else 1 - n).start()
+
+    pl.semaphore_wait(told, 1)
+
+    @pl.when(h == 1)
+    def _():
+        pl.semaphore_signal(told, 1, device_id=sib, device_id_type=MESH)
+
+    for n in range(2):
+        for e in range(2):
+            x_send(e, o, n if e == 0 else 1 - n).start()
+    w_dir = [rc(wrow(k), wa.at[y, h], ss.at[0], wr.at[y, h], {"ri": yn[e], "ro": k}) for n in range(2) for e in range(2) for k in [h if n == e else o]]
 
     def rest(ring_s, fin, ls, outs, ads):
         w_d2d = rc(wrow(o), wa.at[y, h], ss.at[2], wr.at[y, h], sib)
         g_loc = lc(g, gv.at[h], ls.at[0])
         g_d2d = rc(g, gv.at[h], ss.at[3], dr.at[0], sib)
-        x_d2d = [rc(xcols(i, o), xa.at[c, h, i], ss.at[4], xr.at[c, h], sib) for i in range(2)]
+        x_d2d = [rc(xcols(i, o), xa.at[c, h, i], ss.at[4], xr.at[c, h, i], sib) for i in range(2)]
         for cp in [w_d2d, g_loc, g_d2d] + x_d2d:
             cp.start()
-        heard(1)
         for cp in w_dir:
             cp.start()
 
         w_fwd = [rc(wa.at[yn[1 - e], k], wa.at[yn[1 - e], k], ss.at[0], wr.at[yn[1 - e], k], {"ri": yn[e]}) for e, k in ((0, h), (1, o))]
-        x_fwd = [rc(xa.at[cn[1 - e], k], xa.at[cn[1 - e], k], ss.at[1], xr.at[cn[1 - e], k], {"co": cn[e]}) for e, k in ((0, h), (1, o))]
+        x_fwd = [rc(xa.at[cn[1 - e], t, e], xa.at[cn[1 - e], t, e], ss.at[1], xr.at[cn[1 - e], t, e], {"co": cn[e]}) for e in range(2) for t in range(2)]
 
         def got_w(yy, k):
             done(wa.at[yy, k], wr.at[yy, k])
 
-        def got_x(cc, k):
-            done(xa.at[cc, k], xr.at[cc, k])
+        def got_x(cc, i):
+            for t in range(2):
+                done(xa.at[cc, t, i], xr.at[cc, t, i])
 
         def sends(a, part, recv, me, axis, nbr, d):
             k = lax.rem(d - me + 4, 4)
@@ -211,23 +218,26 @@
                     w_fwd[0].start()
                     got_w(yn[0], o)
                     w_fwd[1].start()
-                    got_x(cn[1], h)
+                    got_x(cn[1], 0)
                     x_fwd[0].start()
-                    got_x(cn[0], o)
                     x_fwd[1].start()
+                    got_x(cn[0], 1)
+                    x_fwd[2].start()
+                    x_fwd[3].start()
                     got_w(xor(y, 1), rem1)
 
                 @pl.when(step == 2)
                 def _():
                     x_sends(y // 2)
                     x_sends(2 + y // 2)
-                    got_x(cn[1], o)
-                    got_x(cn[0], h)
+                    got_x(cn[1], 1)
+                    got_x(cn[0], 0)
                     done(xin.at[0], ls.at[2])
 
                 @pl.when(step == 3)
                 def _():
-                    got_x(c, o)
+                    for i in range(2):
+                        done(xa.at[c, o, i], xr.at[c, o, i])
                     got_x(c2, 0)
                     got_x(c2, 1)
 
@@ -266,7 +276,7 @@
         pl.run_scoped(compute, pltpu.VMEM((2 * q, f), BF16), pltpu.VMEM((2, 2, tb, q), BF16), pltpu.VMEM((2, 2 * q, tb), BF16),
                       pltpu.VMEM((2, 2, 2, cr, q), F32), pltpu.VMEM((2, 2, 2, 4, qr, ft), F32))
 
-        def reduce(ax, ay, bx, by, px):
+        def reduce(ax, ay, bx, by, px, sx):
             rings = ((0, pp, rx, c, cn, "co", ax), (1, qq, ry, y, yn, "ri", ay))
 
             @pl.loop(0, 2)
@@ -282,18 +292,29 @@
                         for e in range(2):
                             lc(part.at[nbr[e], e, j], buf.at[e, 0], ads.at[a, 0]).start()
                             lc(recv.at[0, e, j], buf.at[e, 1], ads.at[a, 0]).start()
-                    for a, part, recv, me, nbr, axis, buf in rings:
-                        done(buf.at[:, pl.ds(0, 2)], ads.at[a, 0])
+                    def back(a):
+                        _, part, recv, me, nbr, axis, buf = rings[a]
                         for e in range(2):
                             buf[e, 2] = buf[e, 0] + buf[e, 1]
+                        for e in range(2):
                             lc(buf.at[e, 2], part.at[nbr[e], e, j], ads.at[a, 1]).start()
-                    for a, part, recv, me, nbr, axis, buf in rings:
                         done(buf.at[:, 2], ads.at[a, 1])
+
+                    for a in range(2):
+                        done(rings[a][6].at[:, pl.ds(0, 2)], ads.at[a, 0])
+
+                    @pl.when(n == 0)
+                    def _():
+                        back(0)
 
                     @pl.when(n == 1)
                     def _():
                         for e in range(2):
-                            rc(pp.at[cn[e], e, j], vx.at[e, i], ring_s.at[0], xacc_r.at[e, 1 + i], {"co": cn[e]}).start()
+                            sx[e, i] = ax[e, 0] + ax[e, 1]
+                        for e in range(2):
+                            rc(sx.at[e, i], vx.at[e, i], ring_s.at[0], xacc_r.at[e, 1 + i], {"co": cn[e]}).start()
+
+                    back(1)
 
                 half = pl.ds(n * NH, NH)
 
@@ -383,7 +404,7 @@
             done(rx, ring_s.at[0])
 
         pl.run_scoped(reduce, pltpu.VMEM((2, 3, cr, 2 * q), F32), pltpu.VMEM((2, 3, qr, f), F32),
-                      pltpu.VMEM((2, NH, cr, 2 * q), BF16), pltpu.VMEM((2, NH, qr, f), F32), pltpu.VMEM((2, NH, cr, 2 * q), F32))
+                      pltpu.VMEM((2, NH, cr, 2 * q), BF16), pltpu.VMEM((2, NH, qr, f), F32), pltpu.VMEM((2, NH, cr, 2 * q), F32), pltpu.VMEM((2, NH, cr, 2 * q), F32))
 
     dma = pltpu.SemaphoreType.DMA
     pl.run_scoped(rest, dma((2,)), dma((2,)), dma((4,)), dma((2,)), dma((2, 2)))
@@ -428,7 +449,7 @@
             scratch_shapes=[
                 pltpu.VMEM((2, tb, f), BF16),
                 pltpu.VMEM((2, NH, cr, 2 * q), F32),
-                dma(5), dma(1), dma(4, 2), dma(4, 2), dma(2, 2, 2), dma(2, 2), dma(2, 1 + NH), dma(2, 2), dma(2), pltpu.SemaphoreType.REGULAR,
+                dma(5), dma(1), dma(4, 2), dma(4, 2, 2), dma(2, 2, 2), dma(2, 2), dma(2, 1 + NH), dma(2, 2), dma(2), pltpu.SemaphoreType.REGULAR,
             ],
             compiler_params=pltpu.CompilerParams(collective_id=0, has_side_effects=True, vmem_limit_bytes=52 << 20),
             name="linear_grads",

time: 417 us -> 415 us (level)
  no operation moved by 1% of the time
where the time goes in v5:
time: 415 us; the launch traced here: 414 us
  Pallas kernels  414 us (100%)
    pallas_call x1, Pallas kernels, local_step(): pl.pallas_call(kernel, out_shape=shapes, in_specs=[any_] * 3, out_specs=[...  410 us

profile of v5, /device:TPU:104, one launch (start us, length us, event | category | flops | bytes accessed | tf_op | source)
XLA Modules:
  0.0 414.5 jit_solution(13491662020820720165)
XLA Ops:
  0.6 409.5 %linear_grads.1 = (bf16[2048,1024]{1,0:T(8,128)(2,1)S(1)}, f32[512,3584]{1,0:T(8,128)S(1)}, f32[4,2,8,256,512]{4,3,2,1,0:T(8,128)}, f32[4,2,8,32,3584]{4,3,2,1,0...) custom-call(bf16[2048,1024]{1,0:T(8,128)(2,1)} %x.1, ...), custom_call_target="tpu_custom_call" | custom-call | tf_op jit(solution)/shard_map/linear_grads/pallas_call | solution.py:444
  410.2 4.3 %put.1 = (bf16[2048,1024]{1,0:T(8,128)(2,1)}, f32[512,3584]{1,0:T(8,128)}) custom-call(bf16[2048,1024]{1,0:T(8,128)(2,1)S(1)} %get-tuple-element.4.a, f32[512,3584]{1,0:T(8,128)S(1)} %get-tuple-element.5.b), custom_call_target="tpu_custom_call" | custom-call | tf_op jit(solution)/shard_map/put/pallas_call | solution.py:457

commit v6 on v5

--- a/solution.py
+++ b/solution.py
@@ -14,7 +14,7 @@
 
 
 def kernel(x, w, g, dx, dw, pp, qq, xa, wa, rx, ry, gv, vx,
-           ss, dr, wr, xr, opp_r, pure_r, xacc_r, yacc_r, fin_r, told):
+           ss, dr, xr, fin_r, told, inside):
     h, y, c = lax.axis_index("ro"), lax.axis_index("ri"), lax.axis_index("co")
     o = 1 - h
     tb, dcols = x.shape
@@ -77,16 +77,20 @@
     for n in range(2):
         for e in range(2):
             x_send(e, o, n if e == 0 else 1 - n).start()
-    w_dir = [rc(wrow(k), wa.at[y, h], ss.at[0], wr.at[y, h], {"ri": yn[e], "ro": k}) for n in range(2) for e in range(2) for k in [h if n == e else o]]
-
-    def rest(ring_s, fin, ls, outs, ads):
+
+    def rest(wr, opp_r, pure_r, xacc_r, yacc_r, ring_s, fin, ls, outs, ads):
+        senders = [sib] + [{"ri": yn[e], "ro": k} for e in range(2) for k in range(2)] + [{"co": cn[e]} for e in range(2)]
+        for dev in senders:
+            pl.semaphore_signal(inside, 1, device_id=dev, device_id_type=MESH)
+        w_dir = [rc(wrow(k), wa.at[y, h], ss.at[0], wr.at[y, h], {"ri": yn[e], "ro": k}) for n in range(2) for e in range(2) for k in [h if n == e else o]]
         w_d2d = rc(wrow(o), wa.at[y, h], ss.at[2], wr.at[y, h], sib)
         g_loc = lc(g, gv.at[h], ls.at[0])
         g_d2d = rc(g, gv.at[h], ss.at[3], dr.at[0], sib)
         x_d2d = [rc(xcols(i, o), xa.at[c, h, i], ss.at[4], xr.at[c, h, i], sib) for i in range(2)]
-        for cp in [w_d2d, g_loc, g_d2d] + x_d2d:
+        for cp in [g_loc, g_d2d] + x_d2d:
             cp.start()
-        for cp in w_dir:
+        pl.semaphore_wait(inside, len(senders))
+        for cp in w_dir + [w_d2d]:
             cp.start()
 
         w_fwd = [rc(wa.at[yn[1 - e], k], wa.at[yn[1 - e], k], ss.at[0], wr.at[yn[1 - e], k], {"ri": yn[e]}) for e, k in ((0, h), (1, o))]
@@ -140,10 +144,6 @@
 
                 @pl.loop(0, 8)
                 def _(m):
-                    @pl.when(first & (m == 4))
-                    def _():
-                        done(gv.at[o], dr.at[0])
-
                     s, ab, hf = 1 - m // 4, lax.rem(m // 2, 2), lax.rem(m, 2)
                     t = s * h + (1 - s) * o
                     row = pl.multiple_of(ab * (tb // 2) + hf * (tb // 4), tb // 4)
@@ -206,8 +206,9 @@
             def _(step):
                 @pl.when(step == 0)
                 def _():
+                    got_w(y, o)
+                    done(gv.at[o], dr.at[0])
                     done(gv.at[h], ls.at[0])
-                    got_w(y, o)
 
                 @pl.when(step == 1)
                 def _():
@@ -407,13 +408,13 @@
                       pltpu.VMEM((2, NH, cr, 2 * q), BF16), pltpu.VMEM((2, NH, qr, f), F32), pltpu.VMEM((2, NH, cr, 2 * q), F32), pltpu.VMEM((2, NH, cr, 2 * q), F32))
 
     dma = pltpu.SemaphoreType.DMA
-    pl.run_scoped(rest, dma((2,)), dma((2,)), dma((4,)), dma((2,)), dma((2, 2)))
+    pl.run_scoped(rest, dma((4, 2)), dma((2, 2, 2)), dma((2, 2)), dma((2, 1 + NH)), dma((2, 2)), dma((2,)), dma((2,)), dma((4,)), dma((2,)), dma((2, 2)))
 
 
 def put_kernel(a, b, u, v, sems):
     for i, (src, dst) in enumerate(((b, v), (a, u))):
-        rows = src.shape[0] // 4
-        for n in range(4):
+        rows = src.shape[0] // 8
+        for n in range(8):
             pltpu.make_async_copy(src.at[pl.ds(n * rows, rows)], dst.at[pl.ds(n * rows, rows)], sems.at[i]).start()
     for i, (src, dst) in enumerate(((b, v), (a, u))):
         pltpu.make_async_copy(src, dst, sems.at[i]).wait()
@@ -449,7 +450,7 @@
             scratch_shapes=[
                 pltpu.VMEM((2, tb, f), BF16),
                 pltpu.VMEM((2, NH, cr, 2 * q), F32),
-                dma(5), dma(1), dma(4, 2), dma(4, 2, 2), dma(2, 2, 2), dma(2, 2), dma(2, 1 + NH), dma(2, 2), dma(2), pltpu.SemaphoreType.REGULAR,
+                dma(5), dma(1), dma(4, 2, 2), dma(2), pltpu.SemaphoreType.REGULAR, pltpu.SemaphoreType.REGULAR,
             ],
             compiler_params=pltpu.CompilerParams(collective_id=0, has_side_effects=True, vmem_limit_bytes=52 << 20),
             name="linear_grads",

time: 415 us -> 415 us (level)
  no operation moved by 1% of the time
where the time goes in v6:
time: 415 us; the launch traced here: 414 us
  Pallas kernels  413 us (100%)
    pallas_call x1, Pallas kernels, local_step(): pl.pallas_call(kernel, out_shape=shapes, in_specs=[any_] * 3, out_specs=[...  409 us

profile of v6, /device:TPU:104, one launch (start us, length us, event | category | flops | bytes accessed | tf_op | source)
XLA Modules:
  0.0 414.1 jit_solution(162450175217977675)
XLA Ops:
  0.6 409.2 %linear_grads.1 = (bf16[2048,1024]{1,0:T(8,128)(2,1)S(1)}, f32[512,3584]{1,0:T(8,128)S(1)}, f32[4,2,8,256,512]{4,3,2,1,0:T(8,128)}, f32[4,2,8,32,3584]{4,3,2,1,0...) custom-call(bf16[2048,1024]{1,0:T(8,128)(2,1)} %x.1, ...), custom_call_target="tpu_custom_call" | custom-call | tf_op jit(solution)/shard_map/linear_grads/pallas_call | solution.py:445
  409.9 4.3 %put.1 = (bf16[2048,1024]{1,0:T(8,128)(2,1)}, f32[512,3584]{1,0:T(8,128)}) custom-call(bf16[2048,1024]{1,0:T(8,128)(2,1)S(1)} %get-tuple-element.4.a, f32[512,3584]{1,0:T(8,128)S(1)} %get-tuple-element.5.b), custom_call_target="tpu_custom_call" | custom-call | tf_op jit(solution)/shard_map/put/pallas_call | solution.py:458

commit v7 on v6

--- a/solution.py
+++ b/solution.py
@@ -14,7 +14,7 @@
 
 
 def kernel(x, w, g, dx, dw, pp, qq, xa, wa, rx, ry, gv, vx,
-           ss, dr, xr, fin_r, told, inside):
+           xs, xr, told, inside):
     h, y, c = lax.axis_index("ro"), lax.axis_index("ri"), lax.axis_index("co")
     o = 1 - h
     tb, dcols = x.shape
@@ -39,6 +39,12 @@
     def xor(a, b):
         return 2 * lax.rem(a // 2 + b // 2, 2) + lax.rem(lax.rem(a, 2) + lax.rem(b, 2), 2)
 
+    def xcols(i, k):
+        return x.at[:, pl.ds(pl.multiple_of(i * 2 * q + k * q, q), q)]
+
+    def wrow(k):
+        return w.at[pl.ds(pl.multiple_of(k * q, q), q)]
+
     bar = pltpu.get_barrier_semaphore()
     for e in range(2):
         pl.semaphore_signal(bar, 1, device_id={"co": cn[e]}, device_id_type=MESH)
@@ -55,14 +61,8 @@
         pl.semaphore_wait(bar, 7)
         pl.semaphore_signal(told, 1, device_id=sib, device_id_type=MESH)
 
-    def xcols(i, k):
-        return x.at[:, pl.ds(pl.multiple_of(i * 2 * q + k * q, q), q)]
-
-    def wrow(k):
-        return w.at[pl.ds(pl.multiple_of(k * q, q), q)]
-
     def x_send(e, k, i):
-        return rc(xcols(i, k), xa.at[c, h, i], ss.at[1], xr.at[c, h, i], {"co": cn[e], "ro": k})
+        return rc(xcols(i, k), xa.at[c, h, i], xs.at[0], xr.at[c, h, i], {"co": cn[e], "ro": k})
 
     for n in range(2):
         for e in range(2):
@@ -78,7 +78,7 @@
         for e in range(2):
             x_send(e, o, n if e == 0 else 1 - n).start()
 
-    def rest(wr, opp_r, pure_r, xacc_r, yacc_r, ring_s, fin, ls, outs, ads):
+    def rest(wr, dr, opp_r, pure_r, xacc_r, yacc_r, fin_r, ss, ring_s, fin, ls, outs, ads):
         senders = [sib] + [{"ri": yn[e], "ro": k} for e in range(2) for k in range(2)] + [{"co": cn[e]} for e in range(2)]
         for dev in senders:
             pl.semaphore_signal(inside, 1, device_id=dev, device_id_type=MESH)
@@ -86,15 +86,15 @@
         w_d2d = rc(wrow(o), wa.at[y, h], ss.at[2], wr.at[y, h], sib)
         g_loc = lc(g, gv.at[h], ls.at[0])
         g_d2d = rc(g, gv.at[h], ss.at[3], dr.at[0], sib)
-        x_d2d = [rc(xcols(i, o), xa.at[c, h, i], ss.at[4], xr.at[c, h, i], sib) for i in range(2)]
-        for cp in [g_loc, g_d2d] + x_d2d:
+        x_d2d = [rc(xcols(i, o), xa.at[c, h, i], ss.at[1], xr.at[c, h, i], sib) for i in range(2)]
+        for cp in [g_loc] + x_d2d:
             cp.start()
         pl.semaphore_wait(inside, len(senders))
-        for cp in w_dir + [w_d2d]:
+        for cp in w_dir + [w_d2d, g_d2d]:
             cp.start()
 
         w_fwd = [rc(wa.at[yn[1 - e], k], wa.at[yn[1 - e], k], ss.at[0], wr.at[yn[1 - e], k], {"ri": yn[e]}) for e, k in ((0, h), (1, o))]
-        x_fwd = [rc(xa.at[cn[1 - e], t, e], xa.at[cn[1 - e], t, e], ss.at[1], xr.at[cn[1 - e], t, e], {"co": cn[e]}) for e in range(2) for t in range(2)]
+        x_fwd = [rc(xa.at[cn[1 - e], t, e], xa.at[cn[1 - e], t, e], xs.at[0], xr.at[cn[1 - e], t, e], {"co": cn[e]}) for e in range(2) for t in range(2)]
 
         def got_w(yy, k):
             done(wa.at[yy, k], wr.at[yy, k])
@@ -123,23 +123,16 @@
 
         def compute(wv, xin, xt, pst, qst):
             for i in range(2):
-                lc(xcols(i, h), xin.at[0, i], ls.at[2]).start()
+                lc(xcols(i, h), xin.at[0, i], ls.at[3]).start()
 
             def p_out(slot, r, yy, m):
                 s, ab, hf = 1 - m // 4, lax.rem(m // 2, 2), lax.rem(m, 2)
                 return lc(pst.at[slot, r], pp.at[2 * r + yy // 2, ab, pl.ds(s * 4 + hf * 2, 2), :, pl.ds(pl.multiple_of(lax.rem(yy, 2) * q, q), q)], outs.at[slot])
 
-            def p_step(yy, first):
-                @pl.when(first)
-                def _():
-                    lc(wrow(h), wv.at[pl.ds(pl.multiple_of(h * q, q), q)], ls.at[1]).start()
-                    lc(wa.at[yy, o], wv.at[pl.ds(pl.multiple_of(o * q, q), q)], ls.at[1]).start()
-
-                @pl.when(jnp.logical_not(first))
-                def _():
-                    for r in range(2):
-                        lc(wa.at[yy, r], wv.at[pl.ds(r * q, q)], ls.at[1]).start()
-
+            def load_w(yy, r):
+                lc(wa.at[yy, r], wv.at[pl.ds(pl.multiple_of(r * q, q), q)], ls.at[1]).start()
+
+            def p_step(yy):
                 done(wv, ls.at[1])
 
                 @pl.loop(0, 8)
@@ -166,11 +159,17 @@
                 s = r * h + (1 - r) * o
                 return lc(qst.at[slot, r], qq.at[yy, :, pl.ds(s * 4, 4), :, pl.ds(pl.multiple_of(n * ft, ft), ft)], outs.at[slot])
 
-            def q_step(yy):
+            def load_x(yy):
                 for r in range(2):
                     for t in range(2):
-                        lc(xa.at[2 * r + yy // 2, t, lax.rem(yy, 2)], xin.at[r, t], ls.at[3]).start()
-                done(xin, ls.at[3])
+                        lc(xa.at[2 * r + yy // 2, t, lax.rem(yy, 2)], xin.at[r, t], ls.at[4]).start()
+
+            def q_step(yy, yy_next, qn):
+                @pl.when(qn < 2)
+                def _():
+                    load_x(yy)
+
+                done(xin, ls.at[4])
 
                 @pl.loop(0, NC)
                 def _(n):
@@ -179,6 +178,10 @@
                         for t in range(2):
                             xt[t, r * q:(r + 1) * q, at] = xin[r, t, at, :].T
 
+                @pl.when((qn == 1) | (qn == 2))
+                def _():
+                    load_x(yy_next)
+
                 @pl.loop(0, 7)
                 def _(n):
                     slot = lax.rem(n, 2)
@@ -199,6 +202,10 @@
                     done(qst.at[slot], outs.at[slot])
 
             op = lax.rem(y // 2 + c + 1, 2)
+
+            def qcode(n):
+                return op * ((1 - n // 2) * (2 + n) + n // 2 * (3 - n)) + (1 - op) * lax.rem(n + 1, 4)
+
             even = 1 - lax.rem(y, 2)
             rem1 = even * h + (1 - even) * o
 
@@ -206,15 +213,17 @@
             def _(step):
                 @pl.when(step == 0)
                 def _():
+                    lc(wrow(h), wv.at[pl.ds(pl.multiple_of(h * q, q), q)], ls.at[1]).start()
                     got_w(y, o)
+                    load_w(y, o)
                     done(gv.at[o], dr.at[0])
                     done(gv.at[h], ls.at[0])
 
                 @pl.when(step == 1)
                 def _():
-                    done(xin.at[0], ls.at[2])
+                    done(xin.at[0], ls.at[3])
                     for i in range(2):
-                        lc(xin.at[0, i], xa.at[c, h, i], ls.at[2]).start()
+                        lc(xin.at[0, i], xa.at[c, h, i], ls.at[3]).start()
                     got_w(yn[1], h)
                     w_fwd[0].start()
                     got_w(yn[0], o)
@@ -225,7 +234,9 @@
                     got_x(cn[0], 1)
                     x_fwd[2].start()
                     x_fwd[3].start()
+                    load_w(xor(y, 1), 1 - rem1)
                     got_w(xor(y, 1), rem1)
+                    load_w(xor(y, 1), rem1)
 
                 @pl.when(step == 2)
                 def _():
@@ -233,7 +244,7 @@
                     x_sends(2 + y // 2)
                     got_x(cn[1], 1)
                     got_x(cn[0], 0)
-                    done(xin.at[0], ls.at[2])
+                    done(xin.at[0], ls.at[3])
 
                 @pl.when(step == 3)
                 def _():
@@ -241,32 +252,29 @@
                         done(xa.at[c, o, i], xr.at[c, o, i])
                     got_x(c2, 0)
                     got_x(c2, 1)
-
-                @pl.when(step == 5)
-                def _():
                     got_w(3 - y, 1 - rem1)
+                    for r in range(2):
+                        load_w(3 - y, r)
+                        got_w(y2, r)
 
                 @pl.when(step == 6)
                 def _():
-                    got_w(y2, 0)
-                    got_w(y2, 1)
+                    for r in range(2):
+                        load_w(y2, r)
 
                 late = step // 5
                 is_p = (step < 2) | ((step >= 5) & (step < 7))
                 pn = step - 3 * late
                 qn = step - 2 - 2 * (step // 7)
                 pcode = pn + pn // 2 - 2 * (pn // 3)
-                qa = qn // 2
-                qcode = op * ((1 - qa) * (2 + qn) + qa * (3 - qn)) + (1 - op) * lax.rem(qn + 1, 4)
-
                 @pl.when(is_p)
                 def _():
-                    p_step(xor(y, pcode), step == 0)
+                    p_step(xor(y, pcode))
 
                 @pl.when(jnp.logical_not(is_p))
                 def _():
-                    yy = xor(y, qcode)
-                    q_step(yy)
+                    yy = xor(y, qcode(qn))
+                    q_step(yy, xor(y, qcode(lax.rem(qn + 1, 4))), qn)
                     y_sends(yy)
 
                 @pl.when(step == 6)
@@ -279,6 +287,18 @@
 
         def reduce(ax, ay, bx, by, px, sx):
             rings = ((0, pp, rx, c, cn, "co", ax), (1, qq, ry, y, yn, "ri", ay))
+
+            def x_at(e, j, i):
+                return (pl.ds(pl.multiple_of(e * (tb // 2) + j * cr, cr), cr), pl.ds(pl.multiple_of(i * 2 * q + h * q, q), q))
+
+            def y_at(e, j):
+                return pl.ds(pl.multiple_of(h * q + e * (q // 2) + j * qr, qr), qr)
+
+            for e in range(2):
+                lc(pp.at[c, e, pl.ds(NH, NH)], px.at[e], ls.at[0]).start()
+                lc(qq.at[y, e, pl.ds(0, NH)], by.at[e], ls.at[1]).start()
+                for j in range(NH):
+                    lc(qq.at[y, e, NH + j], dw.at[y_at(e, j)], ls.at[2]).start()
 
             @pl.loop(0, 2)
             def _(n):
@@ -327,56 +347,53 @@
                 for e in range(2):
                     rc(qq.at[yn[e], e, half], ry.at[2, e, half], ring_s.at[1], yacc_r.at[e, n], {"ri": yn[e]}).start()
 
-            def x_at(e, j, i):
-                return (pl.ds(pl.multiple_of(e * (tb // 2) + j * cr, cr), cr), pl.ds(pl.multiple_of(i * 2 * q + h * q, q), q))
-
-            def y_at(e, j):
-                return pl.ds(pl.multiple_of(h * q + e * (q // 2) + j * qr, qr), qr)
-
-            def load(ring, j, third):
-                a, part, recv, me, nbr, axis, buf = ring
-                for e in range(2):
-                    lc(part.at[me, e, j], buf.at[e, 0], ads.at[a, 0]).start()
-                    lc(recv.at[1, 1 - e, j], buf.at[e, 1], ads.at[a, 0]).start()
-                    if third:
-                        lc(recv.at[2, e, j], buf.at[e, 2], ads.at[a, 0]).start()
-                done(buf if third else buf.at[:, pl.ds(0, 2)], ads.at[a, 0])
-
             for a, part, recv, me, nbr, axis, buf in rings:
                 for e in range(2):
                     done(recv.at[1, e], pure_r.at[a, e])
             done(wa.at[pl.ds(0, 3)], ss.at[0])
-            done(xa.at[pl.ds(0, 3)], ss.at[1])
+            done(xa.at[pl.ds(0, 3)], xs.at[0])
             done(wa.at[0, 0], ss.at[2])
             done(gv.at[0], ss.at[3])
-            done(xa.at[0, 0], ss.at[4])
+            done(xa.at[0, 0], ss.at[1])
+
+            done(px, ls.at[0])
+            done(by, ls.at[1])
+            done(by, ls.at[2])
 
             for e in range(2):
                 done(ry.at[2, e, pl.ds(0, NH)], yacc_r.at[e, 0])
 
             @pl.loop(0, NH)
             def _(j):
-                load(rings[1], j, True)
-                for e in range(2):
-                    by[e, j] = ay[e, 0] + ay[e, 1] + ay[e, 2]
+                for e in range(2):
+                    lc(ry.at[1, 1 - e, NH + j], ay.at[e, 0], ads.at[1, 0]).start()
+                    lc(ry.at[1, 1 - e, j], ay.at[e, 1], ads.at[1, 0]).start()
+                    lc(ry.at[2, e, j], ay.at[e, 2], ads.at[1, 0]).start()
+                    lc(rx.at[1, 1 - e, NH + j], ax.at[e, 0], ads.at[0, 0]).start()
+                done(ay, ads.at[1, 0])
+                for e in range(2):
+                    by[e, j] = by[e, j] + ay[e, 1] + ay[e, 2]
                     rc(by.at[e, j], dw.at[y_at(e, j)], fin.at[1], fin_r.at[1], sib).start()
-                load(rings[1], NH + j, False)
-                for e in range(2):
-                    dw[y_at(e, j)] = ay[e, 0] + ay[e, 1]
+                for e in range(2):
+                    dw[y_at(e, j)] += ay[e, 0]
+                done(ax.at[:, 0], ads.at[0, 0])
+                for e in range(2):
+                    px[e, j] += ax[e, 0]
 
             for e in range(2):
                 done(rx.at[2, e, pl.ds(0, NH)], xacc_r.at[e, 0])
 
             @pl.loop(0, NH)
             def _(j):
-                load(rings[0], j, True)
+                for e in range(2):
+                    lc(pp.at[c, e, j], ax.at[e, 0], ads.at[0, 0]).start()
+                    lc(rx.at[1, 1 - e, j], ax.at[e, 1], ads.at[0, 0]).start()
+                    lc(rx.at[2, e, j], ax.at[e, 2], ads.at[0, 0]).start()
+                done(ax, ads.at[0, 0])
                 for e in range(2):
                     bx[e, j] = (ax[e, 0] + ax[e, 1] + ax[e, 2]).astype(BF16)
                     for i in range(2):
                         rc(bx.at[e, j, :, i * q:(i + 1) * q], dx.at[x_at(e, j, i)], fin.at[0], fin_r.at[0], sib).start()
-                load(rings[0], NH + j, False)
-                for e in range(2):
-                    px[e, j] = ax[e, 0] + ax[e, 1]
 
             for e in range(2):
                 done(ry.at[2, e, pl.ds(0, NH)], yacc_r.at[e, 1])
@@ -408,7 +425,7 @@
                       pltpu.VMEM((2, NH, cr, 2 * q), BF16), pltpu.VMEM((2, NH, qr, f), F32), pltpu.VMEM((2, NH, cr, 2 * q), F32), pltpu.VMEM((2, NH, cr, 2 * q), F32))
 
     dma = pltpu.SemaphoreType.DMA
-    pl.run_scoped(rest, dma((4, 2)), dma((2, 2, 2)), dma((2, 2)), dma((2, 1 + NH)), dma((2, 2)), dma((2,)), dma((2,)), dma((4,)), dma((2,)), dma((2, 2)))
+    pl.run_scoped(rest, dma((4, 2)), dma((1,)), dma((2, 2, 2)), dma((2, 2)), dma((2, 1 + NH)), dma((2, 2)), dma((2,)), dma((4,)), dma((2,)), dma((2,)), dma((5,)), dma((2,)), dma((2, 2)))
 
 
 def put_kernel(a, b, u, v, sems):
@@ -450,7 +467,7 @@
             scratch_shapes=[
                 pltpu.VMEM((2, tb, f), BF16),
                 pltpu.VMEM((2, NH, cr, 2 * q), F32),
-                dma(5), dma(1), dma(4, 2, 2), dma(2), pltpu.SemaphoreType.REGULAR, pltpu.SemaphoreType.REGULAR,
+                dma(1), dma(4, 2, 2), pltpu.SemaphoreType.REGULAR, pltpu.SemaphoreType.REGULAR,
             ],
             compiler_params=pltpu.CompilerParams(collective_id=0, has_side_effects=True, vmem_limit_bytes=52 << 20),
             name="linear_grads",

time: 415 us -> 414 us (level)
  no operation moved by 1% of the time
where the time goes in v7:
time: 414 us
  Pallas kernels  413 us (100%)
    pallas_call x1, Pallas kernels, local_step(): pl.pallas_call(kernel, out_shape=shapes, in_specs=[any_] * 3, out_specs=[...  409 us

profile of v7, /device:TPU:104, one launch (start us, length us, event | category | flops | bytes accessed | tf_op | source)
XLA Modules:
  0.0 414.0 jit_solution(7354152242842208531)
XLA Ops:
  0.6 409.2 %linear_grads.1 = (bf16[2048,1024]{1,0:T(8,128)(2,1)S(1)}, f32[512,3584]{1,0:T(8,128)S(1)}, f32[4,2,8,256,512]{4,3,2,1,0:T(8,128)}, f32[4,2,8,32,3584]{4,3,2,1,0...) custom-call(bf16[2048,1024]{1,0:T(8,128)(2,1)} %x.1, ...), custom_call_target="tpu_custom_call" | custom-call | tf_op jit(solution)/shard_map/linear_grads/pallas_call | solution.py:462
  409.8 4.3 %put.1 = (bf16[2048,1024]{1,0:T(8,128)(2,1)}, f32[512,3584]{1,0:T(8,128)}) custom-call(bf16[2048,1024]{1,0:T(8,128)(2,1)S(1)} %get-tuple-element.4.a, f32[512,3584]{1,0:T(8,128)S(1)} %get-tuple-element.5.b), custom_call_target="tpu_custom_call" | custom-call | tf_op jit(solution)/shard_map/put/pallas_call | solution.py:475

commit v8 on v7

--- a/solution.py
+++ b/solution.py
@@ -13,8 +13,8 @@
 NH = NC // 2
 
 
-def kernel(x, w, g, dx, dw, pp, qq, xa, wa, rx, ry, gv, vx,
-           xs, xr, told, inside):
+def kernel(x, w, g, dx, dw, pp, qq, xa, wa, rx, ry, vx,
+           xs, xr, told, inside, ready):
     h, y, c = lax.axis_index("ro"), lax.axis_index("ri"), lax.axis_index("co")
     o = 1 - h
     tb, dcols = x.shape
@@ -84,13 +84,11 @@
             pl.semaphore_signal(inside, 1, device_id=dev, device_id_type=MESH)
         w_dir = [rc(wrow(k), wa.at[y, h], ss.at[0], wr.at[y, h], {"ri": yn[e], "ro": k}) for n in range(2) for e in range(2) for k in [h if n == e else o]]
         w_d2d = rc(wrow(o), wa.at[y, h], ss.at[2], wr.at[y, h], sib)
-        g_loc = lc(g, gv.at[h], ls.at[0])
-        g_d2d = rc(g, gv.at[h], ss.at[3], dr.at[0], sib)
         x_d2d = [rc(xcols(i, o), xa.at[c, h, i], ss.at[1], xr.at[c, h, i], sib) for i in range(2)]
-        for cp in [g_loc] + x_d2d:
+        for cp in x_d2d:
             cp.start()
         pl.semaphore_wait(inside, len(senders))
-        for cp in w_dir + [w_d2d, g_d2d]:
+        for cp in w_dir + [w_d2d]:
             cp.start()
 
         w_fwd = [rc(wa.at[yn[1 - e], k], wa.at[yn[1 - e], k], ss.at[0], wr.at[yn[1 - e], k], {"ri": yn[e]}) for e, k in ((0, h), (1, o))]
@@ -121,7 +119,11 @@
         x_sends = functools.partial(sends, 0, pp, rx, c, "co", cn)
         y_sends = functools.partial(sends, 1, qq, ry, y, "ri", yn)
 
-        def compute(wv, xin, xt, pst, qst):
+        def compute(gv, wv, xin, xt, pst, qst):
+            pl.semaphore_signal(ready, 1, device_id=sib, device_id_type=MESH)
+            lc(g, gv.at[h], ls.at[0]).start()
+            pl.semaphore_wait(ready, 1)
+            rc(g, gv.at[h], ss.at[3], dr.at[0], sib).start()
             for i in range(2):
                 lc(xcols(i, h), xin.at[0, i], ls.at[3]).start()
 
@@ -282,11 +284,12 @@
                     x_sends(1 - y // 2)
                     x_sends(3 - y // 2)
 
-        pl.run_scoped(compute, pltpu.VMEM((2 * q, f), BF16), pltpu.VMEM((2, 2, tb, q), BF16), pltpu.VMEM((2, 2 * q, tb), BF16),
+        pl.run_scoped(compute, pltpu.VMEM((2, tb, f), BF16), pltpu.VMEM((2 * q, f), BF16), pltpu.VMEM((2, 2, tb, q), BF16), pltpu.VMEM((2, 2 * q, tb), BF16),
                       pltpu.VMEM((2, 2, 2, cr, q), F32), pltpu.VMEM((2, 2, 2, 4, qr, ft), F32))
 
-        def reduce(ax, ay, bx, by, px, sx):
-            rings = ((0, pp, rx, c, cn, "co", ax), (1, qq, ry, y, yn, "ri", ay))
+        def reduce(accx, tmpx, nxtx, ownx, sibx, outx, accy, tmpy, nxty, siby):
+            rings = ((0, pp, rx, c, cn, "co", accx, tmpx, nxtx), (1, qq, ry, y, yn, "ri", accy, tmpy, nxty))
+            low, high = pl.ds(0, NH), pl.ds(NH, NH)
 
             def x_at(e, j, i):
                 return (pl.ds(pl.multiple_of(e * (tb // 2) + j * cr, cr), cr), pl.ds(pl.multiple_of(i * 2 * q + h * q, q), q))
@@ -294,119 +297,123 @@
             def y_at(e, j):
                 return pl.ds(pl.multiple_of(h * q + e * (q // 2) + j * qr, qr), qr)
 
-            for e in range(2):
-                lc(pp.at[c, e, pl.ds(NH, NH)], px.at[e], ls.at[0]).start()
-                lc(qq.at[y, e, pl.ds(0, NH)], by.at[e], ls.at[1]).start()
+            for a, part, recv, me, nbr, axis, acc, tmp, nxt in rings:
+                for e in range(2):
+                    lc(part.at[nbr[e], e], acc.at[e], ls.at[a]).start()
+            for e in range(2):
+                lc(pp.at[c, e, low], sibx.at[e], ls.at[2]).start()
+                lc(pp.at[c, e, high], ownx.at[e], ls.at[2]).start()
+                lc(qq.at[y, e, low], siby.at[e], ls.at[3]).start()
                 for j in range(NH):
-                    lc(qq.at[y, e, NH + j], dw.at[y_at(e, j)], ls.at[2]).start()
+                    lc(qq.at[y, e, NH + j], dw.at[y_at(e, j)], ls.at[3]).start()
 
             @pl.loop(0, 2)
             def _(n):
-                for a, part, recv, me, nbr, axis, buf in rings:
+                half = pl.ds(n * NH, NH)
+                for a, part, recv, me, nbr, axis, acc, tmp, nxt in rings:
                     for e in range(2):
-                        done(recv.at[0, e, pl.ds(0, NH)], opp_r.at[a, e, n])
-
-                @pl.loop(0, NH)
-                def _(i):
-                    j = n * NH + i
-                    for a, part, recv, me, nbr, axis, buf in rings:
+                        done(recv.at[0, e, low], opp_r.at[a, e, n])
+                        lc(recv.at[0, e, half], tmp.at[e], ads.at[a]).start()
+
+                @pl.when(n == 0)
+                def _():
+                    done(accx, ls.at[0])
+                    done(accy, ls.at[1])
+
+                for a, part, recv, me, nbr, axis, acc, tmp, nxt in rings:
+                    done(tmp, ads.at[a])
+
+                    @pl.loop(0, NH)
+                    def _(i):
                         for e in range(2):
-                            lc(part.at[nbr[e], e, j], buf.at[e, 0], ads.at[a, 0]).start()
-                            lc(recv.at[0, e, j], buf.at[e, 1], ads.at[a, 0]).start()
-                    def back(a):
-                        _, part, recv, me, nbr, axis, buf = rings[a]
+                            acc[e, n * NH + i] += tmp[e, i]
+
+                @pl.when(n == 0)
+                def _():
+                    for e in range(2):
+                        rc(accx.at[e, low], rx.at[2, e, low], ring_s.at[0], xacc_r.at[e, 0], {"co": cn[e]}).start()
+
+                @pl.when(n == 1)
+                def _():
+                    for i in range(NH):
                         for e in range(2):
-                            buf[e, 2] = buf[e, 0] + buf[e, 1]
-                        for e in range(2):
-                            lc(buf.at[e, 2], part.at[nbr[e], e, j], ads.at[a, 1]).start()
-                        done(buf.at[:, 2], ads.at[a, 1])
-
-                    for a in range(2):
-                        done(rings[a][6].at[:, pl.ds(0, 2)], ads.at[a, 0])
-
-                    @pl.when(n == 0)
-                    def _():
-                        back(0)
-
-                    @pl.when(n == 1)
-                    def _():
-                        for e in range(2):
-                            sx[e, i] = ax[e, 0] + ax[e, 1]
-                        for e in range(2):
-                            rc(sx.at[e, i], vx.at[e, i], ring_s.at[0], xacc_r.at[e, 1 + i], {"co": cn[e]}).start()
-
-                    back(1)
-
-                half = pl.ds(n * NH, NH)
-
-                @pl.when(n == 0)
-                def _():
-                    for e in range(2):
-                        rc(pp.at[cn[e], e, half], rx.at[2, e, half], ring_s.at[0], xacc_r.at[e, 0], {"co": cn[e]}).start()
-
-                for e in range(2):
-                    rc(qq.at[yn[e], e, half], ry.at[2, e, half], ring_s.at[1], yacc_r.at[e, n], {"ri": yn[e]}).start()
-
-            for a, part, recv, me, nbr, axis, buf in rings:
+                            rc(accx.at[e, NH + i], vx.at[e, i], ring_s.at[0], xacc_r.at[e, 1 + i], {"co": cn[e]}).start()
+
+                for e in range(2):
+                    rc(accy.at[e, half], ry.at[2, e, half], ring_s.at[1], yacc_r.at[e, n], {"ri": yn[e]}).start()
+
+            for a, part, recv, me, nbr, axis, acc, tmp, nxt in rings:
                 for e in range(2):
                     done(recv.at[1, e], pure_r.at[a, e])
+                for e in range(2):
+                    lc(recv.at[1, 1 - e, low], tmp.at[e], ads.at[a]).start()
+                    lc(recv.at[1, 1 - e, high], nxt.at[e], ads.at[a]).start()
             done(wa.at[pl.ds(0, 3)], ss.at[0])
             done(xa.at[pl.ds(0, 3)], xs.at[0])
             done(wa.at[0, 0], ss.at[2])
-            done(gv.at[0], ss.at[3])
+            done(g, ss.at[3])
             done(xa.at[0, 0], ss.at[1])
-
-            done(px, ls.at[0])
-            done(by, ls.at[1])
-            done(by, ls.at[2])
-
-            for e in range(2):
-                done(ry.at[2, e, pl.ds(0, NH)], yacc_r.at[e, 0])
+            done(accx, ls.at[2])
+            done(accy, ls.at[3])
+
+            for e in range(2):
+                done(ry.at[2, e, low], yacc_r.at[e, 0])
+            done(accy, ads.at[1])
+
+            @pl.loop(0, NH)
+            def _(i):
+                for e in range(2):
+                    siby[e, i] += tmpy[e, i]
+                    dw[y_at(e, i)] += nxty[e, i]
+
+            for e in range(2):
+                lc(ry.at[2, e, low], tmpy.at[e], ads.at[1]).start()
+            done(accx, ads.at[0])
+
+            @pl.loop(0, NH)
+            def _(i):
+                for e in range(2):
+                    sibx[e, i] += tmpx[e, i]
+                    ownx[e, i] += nxtx[e, i]
+
+            done(tmpy, ads.at[1])
+
+            @pl.loop(0, NH)
+            def _(i):
+                for e in range(2):
+                    siby[e, i] += tmpy[e, i]
+
+            for e in range(2):
+                for i in range(NH):
+                    rc(siby.at[e, i], dw.at[y_at(e, i)], fin.at[1], fin_r.at[1], sib).start()
+
+            for e in range(2):
+                done(rx.at[2, e, low], xacc_r.at[e, 0])
+                lc(rx.at[2, e, low], tmpx.at[e], ads.at[0]).start()
+            done(tmpx, ads.at[0])
 
             @pl.loop(0, NH)
             def _(j):
                 for e in range(2):
-                    lc(ry.at[1, 1 - e, NH + j], ay.at[e, 0], ads.at[1, 0]).start()
-                    lc(ry.at[1, 1 - e, j], ay.at[e, 1], ads.at[1, 0]).start()
-                    lc(ry.at[2, e, j], ay.at[e, 2], ads.at[1, 0]).start()
-                    lc(rx.at[1, 1 - e, NH + j], ax.at[e, 0], ads.at[0, 0]).start()
-                done(ay, ads.at[1, 0])
-                for e in range(2):
-                    by[e, j] = by[e, j] + ay[e, 1] + ay[e, 2]
-                    rc(by.at[e, j], dw.at[y_at(e, j)], fin.at[1], fin_r.at[1], sib).start()
-                for e in range(2):
-                    dw[y_at(e, j)] += ay[e, 0]
-                done(ax.at[:, 0], ads.at[0, 0])
-                for e in range(2):
-                    px[e, j] += ax[e, 0]
-
-            for e in range(2):
-                done(rx.at[2, e, pl.ds(0, NH)], xacc_r.at[e, 0])
+                    outx[e, j] = (sibx[e, j] + tmpx[e, j]).astype(BF16)
 
             @pl.loop(0, NH)
             def _(j):
                 for e in range(2):
-                    lc(pp.at[c, e, j], ax.at[e, 0], ads.at[0, 0]).start()
-                    lc(rx.at[1, 1 - e, j], ax.at[e, 1], ads.at[0, 0]).start()
-                    lc(rx.at[2, e, j], ax.at[e, 2], ads.at[0, 0]).start()
-                done(ax, ads.at[0, 0])
-                for e in range(2):
-                    bx[e, j] = (ax[e, 0] + ax[e, 1] + ax[e, 2]).astype(BF16)
                     for i in range(2):
-                        rc(bx.at[e, j, :, i * q:(i + 1) * q], dx.at[x_at(e, j, i)], fin.at[0], fin_r.at[0], sib).start()
-
-            for e in range(2):
-                done(ry.at[2, e, pl.ds(0, NH)], yacc_r.at[e, 1])
+                        rc(outx.at[e, j, :, i * q:(i + 1) * q], dx.at[x_at(e, j, i)], fin.at[0], fin_r.at[0], sib).start()
+
+            for e in range(2):
+                done(ry.at[2, e, low], yacc_r.at[e, 1])
+                lc(ry.at[2, e, high], tmpy.at[e], ads.at[1]).start()
+            done(tmpy, ads.at[1])
 
             @pl.loop(0, NH)
             def _(j):
                 for e in range(2):
-                    lc(ry.at[2, e, NH + j], ay.at[e, 2], ads.at[1, 0]).start()
-                done(ay.at[:, 2], ads.at[1, 0])
-                for e in range(2):
-                    dw[y_at(e, j)] += ay[e, 2]
-
-            for n, ref in enumerate((bx, by)):
+                    dw[y_at(e, j)] += tmpy[e, j]
+
+            for n, ref in enumerate((outx, siby)):
                 done(ref, fin.at[n])
                 done(ref, fin_r.at[n])
             done(ry, ring_s.at[1])
@@ -415,17 +422,18 @@
             def _(j):
                 for e in range(2):
                     done(vx.at[e, j], xacc_r.at[e, 1 + j])
-                    tot = px[e, j] + vx[e, j]
+                    tot = ownx[e, j] + vx[e, j]
                     for i in range(2):
                         dx[x_at(e, j, i)] = tot[:, i * q:(i + 1) * q].astype(BF16)
 
             done(rx, ring_s.at[0])
 
-        pl.run_scoped(reduce, pltpu.VMEM((2, 3, cr, 2 * q), F32), pltpu.VMEM((2, 3, qr, f), F32),
-                      pltpu.VMEM((2, NH, cr, 2 * q), BF16), pltpu.VMEM((2, NH, qr, f), F32), pltpu.VMEM((2, NH, cr, 2 * q), F32), pltpu.VMEM((2, NH, cr, 2 * q), F32))
+        x_half, y_half = (2, NH, cr, 2 * q), (2, NH, qr, f)
+        pl.run_scoped(reduce, pltpu.VMEM((2, NC, cr, 2 * q), F32), *[pltpu.VMEM(x_half, F32)] * 4, pltpu.VMEM(x_half, BF16),
+                      pltpu.VMEM((2, NC, qr, f), F32), *[pltpu.VMEM(y_half, F32)] * 3)
 
     dma = pltpu.SemaphoreType.DMA
-    pl.run_scoped(rest, dma((4, 2)), dma((1,)), dma((2, 2, 2)), dma((2, 2)), dma((2, 1 + NH)), dma((2, 2)), dma((2,)), dma((4,)), dma((2,)), dma((2,)), dma((5,)), dma((2,)), dma((2, 2)))
+    pl.run_scoped(rest, dma((4, 2)), dma((1,)), dma((2, 2, 2)), dma((2, 2)), dma((2, 1 + NH)), dma((2, 2)), dma((2,)), dma((4,)), dma((2,)), dma((2,)), dma((5,)), dma((2,)), dma((2,)))
 
 
 def put_kernel(a, b, u, v, sems):
@@ -465,9 +473,8 @@
             in_specs=[any_] * 3,
             out_specs=[vmem] * 2 + [any_] * (len(shapes) - 2),
             scratch_shapes=[
-                pltpu.VMEM((2, tb, f), BF16),
                 pltpu.VMEM((2, NH, cr, 2 * q), F32),
-                dma(1), dma(4, 2, 2), pltpu.SemaphoreType.REGULAR, pltpu.SemaphoreType.REGULAR,
+                dma(1), dma(4, 2, 2), pltpu.SemaphoreType.REGULAR, pltpu.SemaphoreType.REGULAR, pltpu.SemaphoreType.REGULAR,
             ],
             compiler_params=pltpu.CompilerParams(collective_id=0, has_side_effects=True, vmem_limit_bytes=52 << 20),
             name="linear_grads",

time: 414 us -> 414 us (level)
  no operation moved by 1% of the time
where the time goes in v8:
time: 414 us
  Pallas kernels  413 us (100%)
    pallas_call x1, Pallas kernels, local_step(): pl.pallas_call(kernel, out_shape=shapes, in_specs=[any_] * 3, out_specs=[...  409 us

profile of v8, /device:TPU:104, one launch (start us, length us, event | category | flops | bytes accessed | tf_op | source)
XLA Modules:
  0.0 414.1 jit_solution(6331931438570675318)
XLA Ops:
  0.6 409.2 %linear_grads.1 = (bf16[2048,1024]{1,0:T(8,128)(2,1)S(1)}, f32[512,3584]{1,0:T(8,128)S(1)}, f32[4,2,8,256,512]{4,3,2,1,0:T(8,128)}, f32[4,2,8,32,3584]{4,3,2,1,0...) custom-call(bf16[2048,1024]{1,0:T(8,128)(2,1)} %x.1, ...), custom_call_target="tpu_custom_call" | custom-call | tf_op jit(solution)/shard_map/linear_grads/pallas_call | solution.py:470
  409.8 4.3 %put.1 = (bf16[2048,1024]{1,0:T(8,128)(2,1)}, f32[512,3584]{1,0:T(8,128)}) custom-call(bf16[2048,1024]{1,0:T(8,128)(2,1)S(1)} %get-tuple-element.4.a, f32[512,3584]{1,0:T(8,128)S(1)} %get-tuple-element.5.b), custom_call_target="tpu_custom_call" | custom-call | tf_op jit(solution)/shard_map/put/pallas_call | solution.py:482

commit v9 on v8

--- a/solution.py
+++ b/solution.py
@@ -62,7 +62,7 @@
         pl.semaphore_signal(told, 1, device_id=sib, device_id_type=MESH)
 
     def x_send(e, k, i):
-        return rc(xcols(i, k), xa.at[c, h, i], xs.at[0], xr.at[c, h, i], {"co": cn[e], "ro": k})
+        return rc(xcols(i, k), xa.at[c, h, i], xs.at[0], xr.at[e, h, i], {"co": cn[e], "ro": k})
 
     for n in range(2):
         for e in range(2):
@@ -78,28 +78,26 @@
         for e in range(2):
             x_send(e, o, n if e == 0 else 1 - n).start()
 
-    def rest(wr, dr, opp_r, pure_r, xacc_r, yacc_r, fin_r, ss, ring_s, fin, ls, outs, ads):
+    def rest(xf, xd, wr, dr, opp_r, pure_r, xacc_r, yacc_r, fin_r, ss, ring_s, fin, ls, outs, ads):
         senders = [sib] + [{"ri": yn[e], "ro": k} for e in range(2) for k in range(2)] + [{"co": cn[e]} for e in range(2)]
         for dev in senders:
             pl.semaphore_signal(inside, 1, device_id=dev, device_id_type=MESH)
         w_dir = [rc(wrow(k), wa.at[y, h], ss.at[0], wr.at[y, h], {"ri": yn[e], "ro": k}) for n in range(2) for e in range(2) for k in [h if n == e else o]]
         w_d2d = rc(wrow(o), wa.at[y, h], ss.at[2], wr.at[y, h], sib)
-        x_d2d = [rc(xcols(i, o), xa.at[c, h, i], ss.at[1], xr.at[c, h, i], sib) for i in range(2)]
-        for cp in x_d2d:
+        x_d2d = [rc(xcols(i, o), xa.at[c, h, i], ss.at[1], xd.at[0], sib) for i in range(2)]
+        pl.semaphore_wait(inside, len(senders))
+        for cp in w_dir + [w_d2d] + x_d2d:
             cp.start()
-        pl.semaphore_wait(inside, len(senders))
-        for cp in w_dir + [w_d2d]:
-            cp.start()
 
         w_fwd = [rc(wa.at[yn[1 - e], k], wa.at[yn[1 - e], k], ss.at[0], wr.at[yn[1 - e], k], {"ri": yn[e]}) for e, k in ((0, h), (1, o))]
-        x_fwd = [rc(xa.at[cn[1 - e], t, e], xa.at[cn[1 - e], t, e], xs.at[0], xr.at[cn[1 - e], t, e], {"co": cn[e]}) for e in range(2) for t in range(2)]
+        x_fwd = [rc(xa.at[cn[1 - e], t, e], xa.at[cn[1 - e], t, e], xs.at[0], xf.at[t, e], {"co": cn[e]}) for e in range(2) for t in range(2)]
 
         def got_w(yy, k):
             done(wa.at[yy, k], wr.at[yy, k])
 
-        def got_x(cc, i):
+        def got_x(e, i):
             for t in range(2):
-                done(xa.at[cc, t, i], xr.at[cc, t, i])
+                done(xa.at[cn[1 - e], t, i], xr.at[e, t, i])
 
         def sends(a, part, recv, me, axis, nbr, d):
             k = lax.rem(d - me + 4, 4)
@@ -230,10 +228,10 @@
                     w_fwd[0].start()
                     got_w(yn[0], o)
                     w_fwd[1].start()
-                    got_x(cn[1], 0)
+                    got_x(0, 0)
                     x_fwd[0].start()
                     x_fwd[1].start()
-                    got_x(cn[0], 1)
+                    got_x(1, 1)
                     x_fwd[2].start()
                     x_fwd[3].start()
                     load_w(xor(y, 1), 1 - rem1)
@@ -244,16 +242,16 @@
                 def _():
                     x_sends(y // 2)
                     x_sends(2 + y // 2)
-                    got_x(cn[1], 1)
-                    got_x(cn[0], 0)
+                    got_x(0, 1)
+                    got_x(1, 0)
                     done(xin.at[0], ls.at[3])
 
                 @pl.when(step == 3)
                 def _():
-                    for i in range(2):
-                        done(xa.at[c, o, i], xr.at[c, o, i])
-                    got_x(c2, 0)
-                    got_x(c2, 1)
+                    done(xa.at[c, o], xd.at[0])
+                    for t in range(2):
+                        for i in range(2):
+                            done(xa.at[c2, t, i], xf.at[t, i])
                     got_w(3 - y, 1 - rem1)
                     for r in range(2):
                         load_w(3 - y, r)
@@ -310,7 +308,7 @@
             @pl.loop(0, 2)
             def _(n):
                 half = pl.ds(n * NH, NH)
-                for a, part, recv, me, nbr, axis, acc, tmp, nxt in rings:
+                for a, part, recv, me, nbr, axis, acc, tmp, nxt in rings[::-1]:
                     for e in range(2):
                         done(recv.at[0, e, low], opp_r.at[a, e, n])
                         lc(recv.at[0, e, half], tmp.at[e], ads.at[a]).start()
@@ -342,7 +340,7 @@
                 for e in range(2):
                     rc(accy.at[e, half], ry.at[2, e, half], ring_s.at[1], yacc_r.at[e, n], {"ri": yn[e]}).start()
 
-            for a, part, recv, me, nbr, axis, acc, tmp, nxt in rings:
+            for a, part, recv, me, nbr, axis, acc, tmp, nxt in rings[::-1]:
                 for e in range(2):
                     done(recv.at[1, e], pure_r.at[a, e])
                 for e in range(2):
@@ -433,7 +431,7 @@
                       pltpu.VMEM((2, NC, qr, f), F32), *[pltpu.VMEM(y_half, F32)] * 3)
 
     dma = pltpu.SemaphoreType.DMA
-    pl.run_scoped(rest, dma((4, 2)), dma((1,)), dma((2, 2, 2)), dma((2, 2)), dma((2, 1 + NH)), dma((2, 2)), dma((2,)), dma((4,)), dma((2,)), dma((2,)), dma((5,)), dma((2,)), dma((2,)))
+    pl.run_scoped(rest, dma((2, 2)), dma((1,)), dma((4, 2)), dma((1,)), dma((2, 2, 2)), dma((2, 2)), dma((2, 1 + NH)), dma((2, 2)), dma((2,)), dma((4,)), dma((2,)), dma((2,)), dma((5,)), dma((2,)), dma((2,)))
 
 
 def put_kernel(a, b, u, v, sems):
@@ -474,7 +472,7 @@
             out_specs=[vmem] * 2 + [any_] * (len(shapes) - 2),
             scratch_shapes=[
                 pltpu.VMEM((2, NH, cr, 2 * q), F32),
-                dma(1), dma(4, 2, 2), pltpu.SemaphoreType.REGULAR, pltpu.SemaphoreType.REGULAR, pltpu.SemaphoreType.REGULAR,
+                dma(1), dma(2, 2, 2), pltpu.SemaphoreType.REGULAR, pltpu.SemaphoreType.REGULAR, pltpu.SemaphoreType.REGULAR,
             ],
             compiler_params=pltpu.CompilerParams(collective_id=0, has_side_effects=True, vmem_limit_bytes=52 << 20),
             name="linear_grads",

time: 414 us -> 414 us (level)
  no operation moved by 1% of the time
where the time goes in v9:
time: 414 us
  Pallas kernels  413 us (100%)
    pallas_call x1, Pallas kernels, local_step(): pl.pallas_call(kernel, out_shape=shapes, in_specs=[any_] * 3, out_specs=[...  409 us

profile of v9, /device:TPU:104, one launch (start us, length us, event | category | flops | bytes accessed | tf_op | source)
XLA Modules:
  0.0 414.0 jit_solution(14193134021651810417)
XLA Ops:
  0.6 409.1 %linear_grads.1 = (bf16[2048,1024]{1,0:T(8,128)(2,1)S(1)}, f32[512,3584]{1,0:T(8,128)S(1)}, f32[4,2,8,256,512]{4,3,2,1,0:T(8,128)}, f32[4,2,8,32,3584]{4,3,2,1,0...) custom-call(bf16[2048,1024]{1,0:T(8,128)(2,1)} %x.1, ...), custom_call_target="tpu_custom_call" | custom-call | tf_op jit(solution)/shard_map/linear_grads/pallas_call | solution.py:468
  409.7 4.3 %put.1 = (bf16[2048,1024]{1,0:T(8,128)(2,1)}, f32[512,3584]{1,0:T(8,128)}) custom-call(bf16[2048,1024]{1,0:T(8,128)(2,1)S(1)} %get-tuple-element.4.a, f32[512,3584]{1,0:T(8,128)S(1)} %get-tuple-element.5.b), custom_call_target="tpu_custom_call" | custom-call | tf_op jit(solution)/shard_map/put/pallas_call | solution.py:480

commit v10 on v9

--- a/solution.py
+++ b/solution.py
@@ -436,8 +436,8 @@
 
 def put_kernel(a, b, u, v, sems):
     for i, (src, dst) in enumerate(((b, v), (a, u))):
-        rows = src.shape[0] // 8
-        for n in range(8):
+        rows = src.shape[0] // 16
+        for n in range(16):
             pltpu.make_async_copy(src.at[pl.ds(n * rows, rows)], dst.at[pl.ds(n * rows, rows)], sems.at[i]).start()
     for i, (src, dst) in enumerate(((b, v), (a, u))):
         pltpu.make_async_copy(src, dst, sems.at[i]).wait()

time: 414 us -> 414 us (level)
  no operation moved by 1% of the time
where the time goes in v10:
time: 414 us
  Pallas kernels  413 us (100%)
    pallas_call x1, Pallas kernels, local_step(): pl.pallas_call(kernel, out_shape=shapes, in_specs=[any_] * 3, out_specs=[...  409 us

profile of v10, /device:TPU:104, one launch (start us, length us, event | category | flops | bytes accessed | tf_op | source)
XLA Modules:
  0.0 414.0 jit_solution(6223979260373166248)
XLA Ops:
  0.6 409.1 %linear_grads.1 = (bf16[2048,1024]{1,0:T(8,128)(2,1)S(1)}, f32[512,3584]{1,0:T(8,128)S(1)}, f32[4,2,8,256,512]{4,3,2,1,0:T(8,128)}, f32[4,2,8,32,3584]{4,3,2,1,0...) custom-call(bf16[2048,1024]{1,0:T(8,128)(2,1)} %x.1, ...), custom_call_target="tpu_custom_call" | custom-call | tf_op jit(solution)/shard_map/linear_grads/pallas_call | solution.py:468
  409.7 4.2 %put.1 = (bf16[2048,1024]{1,0:T(8,128)(2,1)}, f32[512,3584]{1,0:T(8,128)}) custom-call(bf16[2048,1024]{1,0:T(8,128)(2,1)S(1)} %get-tuple-element.4.a, f32[512,3584]{1,0:T(8,128)S(1)} %get-tuple-element.5.b), custom_call_target="tpu_custom_call" | custom-call | tf_op jit(solution)/shard_map/put/pallas_call | solution.py:480

commit v11 on v10

--- a/solution.py
+++ b/solution.py
@@ -436,8 +436,8 @@
 
 def put_kernel(a, b, u, v, sems):
     for i, (src, dst) in enumerate(((b, v), (a, u))):
-        rows = src.shape[0] // 16
-        for n in range(16):
+        rows = src.shape[0] // 32
+        for n in range(32):
             pltpu.make_async_copy(src.at[pl.ds(n * rows, rows)], dst.at[pl.ds(n * rows, rows)], sems.at[i]).start()
     for i, (src, dst) in enumerate(((b, v), (a, u))):
         pltpu.make_async_copy(src, dst, sems.at[i]).wait()

time: 414 us -> 414 us (level)
  no operation moved by 1% of the time
where the time goes in v11:
time: 414 us
  Pallas kernels  413 us (100%)
    pallas_call x1, Pallas kernels, local_step(): pl.pallas_call(kernel, out_shape=shapes, in_specs=[any_] * 3, out_specs=[...  409 us

profile of v11, /device:TPU:104, one launch (start us, length us, event | category | flops | bytes accessed | tf_op | source)
XLA Modules:
  0.0 413.9 jit_solution(11665819718928968700)
XLA Ops:
  0.6 409.1 %linear_grads.1 = (bf16[2048,1024]{1,0:T(8,128)(2,1)S(1)}, f32[512,3584]{1,0:T(8,128)S(1)}, f32[4,2,8,256,512]{4,3,2,1,0:T(8,128)}, f32[4,2,8,32,3584]{4,3,2,1,0...) custom-call(bf16[2048,1024]{1,0:T(8,128)(2,1)} %x.1, ...), custom_call_target="tpu_custom_call" | custom-call | tf_op jit(solution)/shard_map/linear_grads/pallas_call | solution.py:468
  409.7 4.2 %put.1 = (bf16[2048,1024]{1,0:T(8,128)(2,1)}, f32[512,3584]{1,0:T(8,128)}) custom-call(bf16[2048,1024]{1,0:T(8,128)(2,1)S(1)} %get-tuple-element.4.a, f32[512,3584]{1,0:T(8,128)S(1)} %get-tuple-element.5.b), custom_call_target="tpu_custom_call" | custom-call | tf_op jit(solution)/shard_map/put/pallas_call | solution.py:480
